TPU v7x, 32 devices: a whole 2x2x4 slice. The times are simulated.
32 devices in a mesh: dp: 2 (over x), vocab: 16 (over z, y, core).
Axes of the slice: x: 2, y: 2, z: 4, core: 2. Of those that a mesh axis runs over, the one named last changes fastest.
Arguments:
- hidden: bfloat16 [1536, 4096], P(('dp', 'vocab')), may hold values from -75 to 75
- embedding: bfloat16 [8192, 4096], P(('dp', 'vocab')), may hold values from -0.5 to 0.5
- targets: int32 [1536], replicated, may hold values from 0 to 8191
Outputs:
- token_loss: float32 [1536], P(('dp', 'vocab'))
- mean_loss: float32 [], replicated
All inputs are finite; a program needn't handle non-finite values.
Results may differ from a plain program's by a relative error of at most 0.00055.
Values may be sent and summed in bfloat16 or wider, within the bound.
No kernel may reach another device: no remote copies, remote signals or barrier semaphores. Data moves between devices by JAX's collectives and lax.ppermute only.
A program may use at most 64 MiB of HBM per device.

v0:
```python
import functools
import math
import random

import jax
import jax.numpy as jnp
from jax import lax
from jax.experimental import pallas as pl
from jax.experimental.pallas import tpu as pltpu
from jax.sharding import Mesh, PartitionSpec as P


AXES = ("dp", "ring", "core")
SEED = 6000647


def plus(at, step, dims):
    return tuple((a + s) % n for a, s, n in zip(at, step, dims))


def minus(at, step, dims):
    return tuple((a - s) % n for a, s, n in zip(at, step, dims))


def hops_of(dims):
    out = []
    for k, n in enumerate(dims):
        for way in sorted({1 % n, -1 % n} - {0}):
            out.append((k, tuple(way if i == k else 0 for i in range(len(dims)))))
    return out


def attempt(dims, seed, tries):
    hops = hops_of(dims)
    total = math.prod(dims)
    cap = -(-(total - 1) // len(dims))
    origin = [tuple(0 for _ in dims)]
    rnd = random.Random(seed)
    lag = rnd.choice((1, 2, 2))
    apart = rnd.random() < 0.7
    left = [tries]

    def extend(k, steps, places, used):
        left[0] -= 1
        if left[0] < 0:
            return None
        if k == total:
            return steps, places
        options = []
        for source in range(max(1, k - lag + 1)):
            for even in hops:
                to_even = plus(places[0][source], even[1], dims)
                if used[0][even[0]] >= cap or to_even in places[0]:
                    continue
                for odd in hops:
                    to_odd = plus(places[1][source], odd[1], dims)
                    if apart and odd[0] == even[0]:
                        continue
                    if used[1][odd[0]] >= cap or to_odd in places[1]:
                        continue
                    if steps and any(h[0] == p[0] for h, p in zip((even, odd), steps[-1][1:])):
                        continue
                    options.append((source, even, odd, to_even, to_odd))
        rnd.shuffle(options)
        options.sort(key=lambda o: o[0] + rnd.random() * 2 * len(dims))
        for source, even, odd, to_even, to_odd in options[:4]:
            now = [list(used[0]), list(used[1])]
            now[0][even[0]] += 1
            now[1][odd[0]] += 1
            found = extend(
                k + 1,
                steps + [(source, even, odd)],
                (places[0] + [to_even], places[1] + [to_odd]),
                now,
            )
            if found:
                return found
        return None

    return extend(1, [], (origin, origin), [[0] * len(dims)] * 2)


def relay(dims, seed=SEED, tries=400):
    while True:
        found = attempt(dims, seed, tries)
        if found:
            return found
        seed += 1


def score_kernel(count, slots, slot_ref, dev_ref, base_ref, *refs):
    blocks = refs[:count]
    mine, theirs, targets, kept, stats = refs[count:]
    tok = blocks[0].shape[0]
    groups = stats.shape[0] // 2
    left = jnp.concatenate([b[...] for b in blocks], axis=0) if count > 1 else blocks[0][...]
    stats[...] = kept[...]
    logits = []
    for table in (mine, theirs):
        logits.append(
            lax.dot_general(
                table[...], left, (((1,), (1,)), ((), ())), preferred_element_type=jnp.float32
            )
        )
    wanted = jnp.concatenate([targets[pl.ds(dev_ref[s], 1), :] for s in slots], axis=1)
    maxima = functools.reduce(jnp.maximum, [jnp.max(x, axis=0, keepdims=True) for x in logits])
    totals = 0.0
    picked = 0.0
    ids = lax.broadcasted_iota(jnp.int32, logits[0].shape, 0)
    for k, x in enumerate(logits):
        totals += jnp.sum(jnp.exp(x - maxima), axis=0, keepdims=True)
        picked += jnp.sum(
            jnp.where(ids == wanted - base_ref[k], x, jnp.zeros_like(x)), axis=0, keepdims=True
        )
    level = maxima + jnp.log(totals)
    for i, s in enumerate(slots):
        at = slot_ref[s]
        stats[pl.ds(at, 1), :] = level[:, i * tok : (i + 1) * tok]
        stats[pl.ds(groups + at, 1), :] = picked[:, i * tok : (i + 1) * tok]


def score(slots, blocks, mine, theirs, targets, kept, slot_of, dev_of, bases):
    count = len(blocks)
    smem = pl.BlockSpec(memory_space=pltpu.SMEM)
    vmem = pl.BlockSpec(memory_space=pltpu.VMEM)
    tok, width = blocks[0].shape
    rows = mine.shape[0] * 2
    return pl.pallas_call(
        functools.partial(score_kernel, count, slots),
        out_shape=jax.ShapeDtypeStruct(kept.shape, jnp.float32),
        in_specs=[smem] * 3 + [vmem] * (count + 4),
        out_specs=vmem,
        cost_estimate=pl.CostEstimate(
            flops=2 * rows * width * tok * count,
            bytes_accessed=2 * width * (rows + tok * count),
            transcendentals=rows * tok * count,
        ),
        compiler_params=pltpu.CompilerParams(vmem_limit_bytes=24 * 1024 * 1024),
        name="score",
    )(slot_of, dev_of, bases, *blocks, mine, theirs, targets, kept)


def batches_of(dims):
    total = math.prod(dims)
    last = total - len(dims)
    edges = (0, (last + 1) // 2, last, total)
    return [tuple(range(low, high)) for low, high in zip(edges[:-1], edges[1:])]


def joined(parts):
    half = parts[0].shape[0] // 2
    levels = [p[:half] for p in parts]
    top = functools.reduce(jnp.maximum, levels)
    total = functools.reduce(jnp.add, [jnp.exp(x - top) for x in levels])
    picked = functools.reduce(jnp.add, [p[half:] for p in parts])
    return jnp.concatenate([top + jnp.log(total), picked], axis=0)


def local(mesh_sizes, dims, hidden, embedding, targets):
    return share(mesh_sizes, dims, hidden, embedding, targets)


def share(mesh_sizes, dims, hidden, embedding, targets):
    dp, ring, cores = mesh_sizes
    chips = dp * ring
    tok = hidden.shape[0]
    rows = embedding.shape[0]
    chip = lax.axis_index("dp") * ring + lax.axis_index("ring")
    core = lax.axis_index("core")
    device = chip * cores + core

    strides = [1] * len(dims)
    for k in reversed(range(len(dims) - 1)):
        strides[k] = strides[k + 1] * dims[k + 1]
    spots = [tuple(i // s % n for s, n in zip(strides, dims)) for i in range(chips)]
    index = {spot: i for i, spot in enumerate(spots)}

    def moved(array, steps, swap=False):
        pairs = []
        for i, spot in enumerate(spots):
            for c in range(cores):
                to = index[plus(spot, steps[c], dims)]
                pairs.append((i * cores + c, to * cores + (cores - 1 - c if swap else c)))
        return lax.ppermute(array, AXES, pairs)

    steps, places = relay(dims)
    still = (tuple(0 for _ in dims),) * cores
    theirs = moved(embedding, still, swap=True)

    owners = jnp.array(
        [[[index[minus(spot, at, dims)] for at in places[c]] for c in range(cores)] for spot in spots],
        jnp.int32,
    )
    slot_of = owners[chip, core]
    dev_of = slot_of * cores + core
    bases = jnp.stack([device * rows, (chip * cores + (cores - 1 - core)) * rows])
    wanted = targets.reshape(chips * cores, tok)

    blocks = [hidden]
    for k, (source, even, odd) in enumerate(steps, 1):
        blocks.append(moved(blocks[source], (even[1], odd[1])))

    stats = jnp.zeros((2 * chips, tok), jnp.float32)
    for slots in batches_of(dims):
        stats = score(
            slots, [blocks[s] for s in slots], embedding, theirs, wanted, stats, slot_of, dev_of, bases
        )

    turns = [plus(still[0], s, dims) for s in spots[1:]]
    along = [t for t in turns if sum(1 for v in t if v) == 1 and t[1]]
    across = [t for t in turns if not t[1]]
    stats = joined([stats] + [moved(stats, (t,) * cores) for t in along])
    stats = joined([stats] + [moved(stats, (t,) * cores) for t in across])
    losses = stats[:chips] - stats[chips:]
    other = moved(losses, still, swap=True)
    mean_loss = (jnp.sum(losses) + jnp.sum(other)) / (tok * chips * cores)
    token_loss = lax.dynamic_slice_in_dim(losses, chip, 1).reshape(tok)
    return token_loss, mean_loss


def gathered(hidden, embedding, targets):
    tok, rows = hidden.shape[0], embedding.shape[0]
    device = lax.axis_index(AXES)
    tokens = lax.all_gather(hidden, AXES, axis=0, tiled=True)
    logits = lax.dot_general(
        tokens, embedding, (((1,), (1,)), ((), ())), preferred_element_type=jnp.float32
    )
    ids = device * rows + jnp.arange(rows, dtype=jnp.int32)
    maxima = lax.pmax(jnp.max(logits, axis=1), AXES)
    totals = jnp.sum(jnp.exp(logits - maxima[:, None]), axis=1)
    picked = jnp.sum(
        jnp.where(targets[:, None] == ids[None, :], logits, jnp.zeros_like(logits)), axis=1
    )
    totals, picked = lax.psum((totals, picked), AXES)
    losses = maxima + jnp.log(totals) - picked
    token_loss = lax.dynamic_slice_in_dim(losses, device * tok, tok)
    return token_loss, jnp.sum(losses) / losses.shape[0]


def solution(mesh):
    dp, vocab = mesh.shape["dp"], mesh.shape["vocab"]
    sizes = (dp, vocab // 2, 2)
    dims = (dp, vocab // 4, 2)
    fine = Mesh(mesh.devices.reshape(sizes), AXES)
    few = dp * vocab <= 64
    return jax.shard_map(
        functools.partial(local, sizes, dims) if few else gathered,
        mesh=fine,
        in_specs=(P(AXES, None), P(AXES, None), P()),
        out_specs=(P(AXES), P()),
        check_vma=False,
    )
```

profile of v0, /device:TPU:0, one launch (start us, length us, event | category | flops | bytes accessed | tf_op | source)
XLA Modules:
  0.0 83.4 jit_solution(5066525983227620945)
XLA Ops:
  1.2 4.7 %collective-permute-start.4 = (bf16[48,4096]{1,0:T(8,128)(2,1)}, bf16[48,4096]{1,0:T(8,128)(2,1)S(1)}, u32[]{:S(2)}, u32[]{:S(2)}) collective-permute-start(bf16[48,4096]{1,0:T(8,128)(2,1)} %refs_0_.1), channel_id=1, source_target_pairs={{0,12},{1,5},{2,14},{3,7},{4,0},{5,9},{6,2},{7,11},{8,4},{9,13},{1... | collective-permute-start | bytes 1179656 | tf_op jit(solution)/shard_map/ppermute | solution.py:184
  5.8 1.5 %collective-permute-start = (bf16[48,4096]{1,0:T(8,128)(2,1)}, bf16[48,4096]{1,0:T(8,128)(2,1)S(1)}, u32[]{:S(2)}, u32[]{:S(2)}) collective-permute-start(bf16[48,4096]{1,0:T(8,128)(2,1)} %refs_0_.1), channel_id=1, source_target_pairs={{0,16},{1,3},{2,18},{3,1},{4,20},{5,7},{6,22},{7,5},{8,24},{9,11},... | collective-permute-start | bytes 1179656 | tf_op jit(solution)/shard_map/ppermute | solution.py:184
  7.3 1.5 %collective-permute-start.15 = (bf16[48,4096]{1,0:T(8,128)(2,1)}, bf16[48,4096]{1,0:T(8,128)(2,1)S(1)}, u32[]{:S(2)}, u32[]{:S(2)}) collective-permute-start(bf16[48,4096]{1,0:T(8,128)(2,1)} %refs_0_.1), channel_id=1, source_target_pairs={{0,2},{1,17},{2,0},{3,19},{4,6},{5,21},{6,4},{7,23},{8,10},{9,25},... | collective-permute-start | bytes 1179656 | tf_op jit(solution)/shard_map/ppermute | solution.py:184
  8.9 7.5 %collective-permute-done.4.refs_2_ = bf16[48,4096]{1,0:T(8,128)(2,1)S(1)} collective-permute-done((bf16[48,4096]{1,0:T(8,128)(2,1)}, bf16[48,4096]{1,0:T(8,128)(2,1)S(1)}, u32[]{:S(2)}, u32[]{:S(2)}) %collective-permute-start.4) | collective-permute-done | bytes 393248 | tf_op jit(solution)/shard_map/ppermute | solution.py:184
  16.3 3.1 %collective-permute-start.14 = (bf16[48,4096]{1,0:T(8,128)(2,1)S(1)}, bf16[48,4096]{1,0:T(8,128)(2,1)S(1)}, u32[]{:S(2)}, u32[]{:S(2)}) collective-permute-start(bf16[48,4096]{1,0:T(8,128)(2,1)S(1)} %collective-permute-done.4.refs_2_), channel_id=1, source_target_pairs={{0,16},{1,3},{2,18},{3,1},{4,20},{5,7},{6,22},{7,5},{8,24},{9,11},... | collective-permute-start | bytes 1179656 | tf_op jit(solution)/shard_map/ppermute | solution.py:184
  19.5 2.4 %collective-permute-start.1 = (bf16[48,4096]{1,0:T(8,128)(2,1)S(1)}, bf16[48,4096]{1,0:T(8,128)(2,1)}, u32[]{:S(2)}, u32[]{:S(2)}) collective-permute-start(bf16[48,4096]{1,0:T(8,128)(2,1)S(1)} %collective-permute-done.refs_1_), channel_id=1, source_target_pairs={{0,2},{1,17},{2,0},{3,19},{4,6},{5,21},{6,4},{7,23},{8,10},{9,25},... | collective-permute-start | bytes 1179656 | tf_op jit(solution)/shard_map/ppermute | solution.py:184
  21.9 2.3 %collective-permute-done.9.refs_4_ = bf16[48,4096]{1,0:T(8,128)(2,1)S(1)} collective-permute-done((bf16[48,4096]{1,0:T(8,128)(2,1)}, bf16[48,4096]{1,0:T(8,128)(2,1)S(1)}, u32[]{:S(2)}, u32[]{:S(2)}) %collective-permute-start.9) | collective-permute-done | bytes 393248 | tf_op jit(solution)/shard_map/ppermute | solution.py:184
  24.2 1.7 %collective-permute-start.5 = (bf16[48,4096]{1,0:T(8,128)(2,1)S(1)}, bf16[48,4096]{1,0:T(8,128)(2,1)S(1)}, u32[]{:S(2)}, u32[]{:S(2)}) collective-permute-start(bf16[48,4096]{1,0:T(8,128)(2,1)S(1)} %collective-permute-done.4.refs_2_), channel_id=1, source_target_pairs={{0,12},{1,5},{2,14},{3,7},{4,0},{5,9},{6,2},{7,11},{8,4},{9,13},{1... | collective-permute-start | bytes 1179656 | tf_op jit(solution)/shard_map/ppermute | solution.py:184
  25.9 0.7 copy-done.3
  26.7 1.5 %collective-permute-start.11 = (bf16[48,4096]{1,0:T(8,128)(2,1)S(1)}, bf16[48,4096]{1,0:T(8,128)(2,1)}, u32[]{:S(2)}, u32[]{:S(2)}) collective-permute-start(bf16[48,4096]{1,0:T(8,128)(2,1)S(1)} %collective-permute-done.4.refs_2_), channel_id=1, source_target_pairs={{0,2},{1,17},{2,0},{3,19},{4,6},{5,21},{6,4},{7,23},{8,10},{9,25},... | collective-permute-start | bytes 1179656 | tf_op jit(solution)/shard_map/ppermute | solution.py:184
  28.2 0.8 copy-done.7
  29.0 1.5 %collective-permute-start.10 = (bf16[48,4096]{1,0:T(8,128)(2,1)S(1)}, bf16[48,4096]{1,0:T(8,128)(2,1)}, u32[]{:S(2)}, u32[]{:S(2)}) collective-permute-start(bf16[48,4096]{1,0:T(8,128)(2,1)S(1)} %collective-permute-done.9.refs_4_), channel_id=1, source_target_pairs={{0,16},{1,3},{2,18},{3,1},{4,20},{5,7},{6,22},{7,5},{8,24},{9,11},... | collective-permute-start | bytes 1179656 | tf_op jit(solution)/shard_map/ppermute | solution.py:184
  30.5 5.4 %collective-permute-start.2 = (bf16[48,4096]{1,0:T(8,128)(2,1)}, bf16[48,4096]{1,0:T(8,128)(2,1)}, u32[]{:S(2)}, u32[]{:S(2)}) collective-permute-start(bf16[48,4096]{1,0:T(8,128)(2,1)} %collective-permute-done.1.refs_3_), channel_id=1, source_target_pairs={{0,4},{1,13},{2,6},{3,15},{4,8},{5,1},{6,10},{7,3},{8,12},{9,5},{1... | collective-permute-start | bytes 1179656 | tf_op jit(solution)/shard_map/ppermute | solution.py:184
  35.8 2.7 %collective-permute-done.5.refs_3_ = bf16[48,4096]{1,0:T(8,128)(2,1)S(1)} collective-permute-done((bf16[48,4096]{1,0:T(8,128)(2,1)S(1)}, bf16[48,4096]{1,0:T(8,128)(2,1)S(1)}, u32[]{:S(2)}, u32[]{:S(2)}) %collective-permute-start.5) | collective-permute-done | bytes 393248 | tf_op jit(solution)/shard_map/ppermute | solution.py:184
  38.6 4.3 %collective-permute-start.12 = (bf16[48,4096]{1,0:T(8,128)(2,1)S(1)}, bf16[48,4096]{1,0:T(8,128)(2,1)}, u32[]{:S(2)}, u32[]{:S(2)}) collective-permute-start(bf16[48,4096]{1,0:T(8,128)(2,1)S(1)} %collective-permute-done.9.refs_4_), channel_id=1, source_target_pairs={{0,2},{1,17},{2,0},{3,19},{4,6},{5,21},{6,4},{7,23},{8,10},{9,25},... | collective-permute-start | bytes 1179656 | tf_op jit(solution)/shard_map/ppermute | solution.py:184
  42.9 0.7 collective-permute-start.6
  43.6 2.0 %collective-permute-done.2.refs_0_ = bf16[48,4096]{1,0:T(8,128)(2,1)} collective-permute-done((bf16[48,4096]{1,0:T(8,128)(2,1)}, bf16[48,4096]{1,0:T(8,128)(2,1)}, u32[]{:S(2)}, u32[]{:S(2)}) %collective-permute-start.2) | collective-permute-done | bytes 393248 | tf_op jit(solution)/shard_map/ppermute | solution.py:184
  46.0 4.2 %collective-permute-start.3 = (bf16[48,4096]{1,0:T(8,128)(2,1)}, bf16[48,4096]{1,0:T(8,128)(2,1)}, u32[]{:S(2)}, u32[]{:S(2)}) collective-permute-start(bf16[48,4096]{1,0:T(8,128)(2,1)} %collective-permute-done.2.refs_0_), channel_id=1, source_target_pairs={{0,4},{1,13},{2,6},{3,15},{4,8},{5,1},{6,10},{7,3},{8,12},{9,5},{1... | collective-permute-start | bytes 1179656 | tf_op jit(solution)/shard_map/ppermute | solution.py:184
  50.2 0.8 reshape.10.refs_9_.refs_8_.refs_5_
  51.0 0.7 multiply_add_fusion
  51.7 1.6 %copy-done = bf16[256,4096]{1,0:T(8,128)(2,1)S(1)} copy-done((bf16[256,4096]{1,0:T(8,128)(2,1)S(1)}, bf16[256,4096]{1,0:T(8,128)(2,1)}, u32[]{:S(2)}) %copy-start) | copy-done | bytes 2097176
  53.3 1.0 %copy-done.2 = bf16[48,4096]{1,0:T(8,128)(2,1)S(1)} copy-done((bf16[48,4096]{1,0:T(8,128)(2,1)S(1)}, bf16[48,4096]{1,0:T(8,128)(2,1)}, u32[]{:S(2)}) %copy-start.2) | copy-done | bytes 393240
  54.3 1.0 %copy-done.4 = bf16[48,4096]{1,0:T(8,128)(2,1)S(1)} copy-done((bf16[48,4096]{1,0:T(8,128)(2,1)S(1)}, bf16[48,4096]{1,0:T(8,128)(2,1)}, u32[]{:S(2)}) %copy-start.4) | copy-done | bytes 393240
  55.3 1.0 %copy-done.8 = bf16[48,4096]{1,0:T(8,128)(2,1)S(1)} copy-done((bf16[48,4096]{1,0:T(8,128)(2,1)S(1)}, bf16[48,4096]{1,0:T(8,128)(2,1)}, u32[]{:S(2)}) %copy-start.8) | copy-done | bytes 393240
  56.3 3.7 %score.3.refs_9_ = f32[32,48]{1,0:T(8,128)S(1)} custom-call(s32[16]{0:T(128)S(1)} %get-tuple-element.5.slot_ref, s32[16]{0:T(128)S(1)} %get-tuple-element.4.dev_ref, s32[2]{0:T(128)S(1)} %pad_add_fusion.base_ref, bf16[48,4096]{1,0:T(8,128)(2,1)S(1)} %copy-done.2, bf16[48,4096]{1,0:T(8,128)(2,1)S(1)} %collective-permute-done.refs_1_, ...), custom_call_target="tpu_custom_call" | custom-call | flops 1409286144 | bytes 6946816 | tf_op jit(solution)/shard_map/score/pallas_call | solution.py:128
  60.0 4.0 %score.4.refs_6_ = f32[32,48]{1,0:T(8,128)S(1)} custom-call(s32[16]{0:T(128)S(1)} %get-tuple-element.5.slot_ref, s32[16]{0:T(128)S(1)} %get-tuple-element.4.dev_ref, s32[2]{0:T(128)S(1)} %pad_add_fusion.base_ref, bf16[48,4096]{1,0:T(8,128)(2,1)} %collective-permute-done.2.refs_0_, bf16[48,4096]{1,0:T(8,128)(2,1)} %collective-permute-done.10.refs_1_, ...), custom_call_target="tpu_custom_call" | custom-call | flops 1207959552 | bytes 6553600 | tf_op jit(solution)/shard_map/score/pallas_call | solution.py:128
  64.0 2.7 %score.5 = f32[32,48]{1,0:T(8,128)S(1)} custom-call(s32[16]{0:T(128)S(1)} %get-tuple-element.5.slot_ref, s32[16]{0:T(128)S(1)} %get-tuple-element.4.dev_ref, s32[2]{0:T(128)S(1)} %pad_add_fusion.base_ref, bf16[48,4096]{1,0:T(8,128)(2,1)} %collective-permute-done.3.refs_0_, bf16[48,4096]{1,0:T(8,128)(2,1)} %collective-permute-done.6.refs_1_, ...), custom_call_target="tpu_custom_call" | custom-call | flops 603979776 | bytes 5373952 | tf_op jit(solution)/shard_map/score/pallas_call | solution.py:128
  67.0 3.6 %collective-permute-start.18 = (f32[32,48]{1,0:T(8,128)S(1)}, f32[32,48]{1,0:T(8,128)S(1)}, u32[]{:S(2)}, u32[]{:S(2)}) collective-permute-start(f32[32,48]{1,0:T(8,128)S(1)} %score.5), channel_id=1, source_target_pairs={{0,12},{1,13},{2,14},{3,15},{4,0},{5,1},{6,2},{7,3},{8,4},{9,5},{1... | collective-permute-start | bytes 18440 | tf_op jit(solution)/shard_map/ppermute | solution.py:184
  70.6 1.7 %collective-permute-done.16 = f32[32,48]{1,0:T(8,128)S(1)} collective-permute-done((f32[32,48]{1,0:T(8,128)S(1)}, f32[32,48]{1,0:T(8,128)S(1)}, u32[]{:S(2)}, u32[]{:S(2)}) %collective-permute-start.16) | collective-permute-done | bytes 6176 | tf_op jit(solution)/shard_map/ppermute | solution.py:184
  73.2 0.7 collective-permute-start.20
  73.9 2.5 %collective-permute-start.21 = (f32[32,48]{1,0:T(8,128)S(1)}, f32[32,48]{1,0:T(8,128)S(1)}, u32[]{:S(2)}, u32[]{:S(2)}) collective-permute-start(f32[32,48]{1,0:T(8,128)S(1)} %pad_maximum_fusion), channel_id=1, source_target_pairs={{0,18},{1,19},{2,16},{3,17},{4,22},{5,23},{6,20},{7,21},{8,26},{9,... | collective-permute-start | bytes 18440 | tf_op jit(solution)/shard_map/ppermute | solution.py:184
  76.9 1.6 %collective-permute-done.21 = f32[32,48]{1,0:T(8,128)S(1)} collective-permute-done((f32[32,48]{1,0:T(8,128)S(1)}, f32[32,48]{1,0:T(8,128)S(1)}, u32[]{:S(2)}, u32[]{:S(2)}) %collective-permute-start.21) | collective-permute-done | bytes 6176 | tf_op jit(solution)/shard_map/ppermute | solution.py:184
  (44 shorter events, 5.1 us)
Async XLA Ops:
  0.6 45.3 %collective-permute-start.8 = (bf16[256,4096]{1,0:T(8,128)(2,1)}, bf16[256,4096]{1,0:T(8,128)(2,1)S(1)}, u32[]{:S(2)}, u32[]{:S(2)}) collective-permute-start(bf16[256,4096]{1,0:T(8,128)(2,1)} %refs_3_.1), channel_id=1, source_target_pairs={{0,1},{1,0},{2,3},{3,2},{4,5},{5,4},{6,7},{7,6},{8,9},{9,8},{10,11... | collective-permute-start | bytes 6291464 | tf_op jit(solution)/shard_map/ppermute | solution.py:184
  1.2 15.1 %collective-permute-start.4 = (bf16[48,4096]{1,0:T(8,128)(2,1)}, bf16[48,4096]{1,0:T(8,128)(2,1)S(1)}, u32[]{:S(2)}, u32[]{:S(2)}) collective-permute-start(bf16[48,4096]{1,0:T(8,128)(2,1)} %refs_0_.1), channel_id=1, source_target_pairs={{0,12},{1,5},{2,14},{3,7},{4,0},{5,9},{6,2},{7,11},{8,4},{9,13},{1... | collective-permute-start | bytes 1179656 | tf_op jit(solution)/shard_map/ppermute | solution.py:184
  5.8 13.6 %collective-permute-start = (bf16[48,4096]{1,0:T(8,128)(2,1)}, bf16[48,4096]{1,0:T(8,128)(2,1)S(1)}, u32[]{:S(2)}, u32[]{:S(2)}) collective-permute-start(bf16[48,4096]{1,0:T(8,128)(2,1)} %refs_0_.1), channel_id=1, source_target_pairs={{0,16},{1,3},{2,18},{3,1},{4,20},{5,7},{6,22},{7,5},{8,24},{9,11},... | collective-permute-start | bytes 1179656 | tf_op jit(solution)/shard_map/ppermute | solution.py:184
  7.3 16.9 %collective-permute-start.9 = (bf16[48,4096]{1,0:T(8,128)(2,1)}, bf16[48,4096]{1,0:T(8,128)(2,1)S(1)}, u32[]{:S(2)}, u32[]{:S(2)}) collective-permute-start(bf16[48,4096]{1,0:T(8,128)(2,1)} %refs_0_.1), channel_id=1, source_target_pairs={{0,4},{1,13},{2,6},{3,15},{4,8},{5,1},{6,10},{7,3},{8,12},{9,5},{1... | collective-permute-start | bytes 1179656 | tf_op jit(solution)/shard_map/ppermute | solution.py:184
  7.3 18.6 %collective-permute-start.15 = (bf16[48,4096]{1,0:T(8,128)(2,1)}, bf16[48,4096]{1,0:T(8,128)(2,1)S(1)}, u32[]{:S(2)}, u32[]{:S(2)}) collective-permute-start(bf16[48,4096]{1,0:T(8,128)(2,1)} %refs_0_.1), channel_id=1, source_target_pairs={{0,2},{1,17},{2,0},{3,19},{4,6},{5,21},{6,4},{7,23},{8,10},{9,25},... | collective-permute-start | bytes 1179656 | tf_op jit(solution)/shard_map/ppermute | solution.py:184
  16.3 11.9 %collective-permute-start.14 = (bf16[48,4096]{1,0:T(8,128)(2,1)S(1)}, bf16[48,4096]{1,0:T(8,128)(2,1)S(1)}, u32[]{:S(2)}, u32[]{:S(2)}) collective-permute-start(bf16[48,4096]{1,0:T(8,128)(2,1)S(1)} %collective-permute-done.4.refs_2_), channel_id=1, source_target_pairs={{0,16},{1,3},{2,18},{3,1},{4,20},{5,7},{6,22},{7,5},{8,24},{9,11},... | collective-permute-start | bytes 1179656 | tf_op jit(solution)/shard_map/ppermute | solution.py:184
  19.5 11.0 %collective-permute-start.1 = (bf16[48,4096]{1,0:T(8,128)(2,1)S(1)}, bf16[48,4096]{1,0:T(8,128)(2,1)}, u32[]{:S(2)}, u32[]{:S(2)}) collective-permute-start(bf16[48,4096]{1,0:T(8,128)(2,1)S(1)} %collective-permute-done.refs_1_), channel_id=1, source_target_pairs={{0,2},{1,17},{2,0},{3,19},{4,6},{5,21},{6,4},{7,23},{8,10},{9,25},... | collective-permute-start | bytes 1179656 | tf_op jit(solution)/shard_map/ppermute | solution.py:184
  24.2 14.4 %collective-permute-start.5 = (bf16[48,4096]{1,0:T(8,128)(2,1)S(1)}, bf16[48,4096]{1,0:T(8,128)(2,1)S(1)}, u32[]{:S(2)}, u32[]{:S(2)}) collective-permute-start(bf16[48,4096]{1,0:T(8,128)(2,1)S(1)} %collective-permute-done.4.refs_2_), channel_id=1, source_target_pairs={{0,12},{1,5},{2,14},{3,7},{4,0},{5,9},{6,2},{7,11},{8,4},{9,13},{1... | collective-permute-start | bytes 1179656 | tf_op jit(solution)/shard_map/ppermute | solution.py:184
  25.9 0.7 copy-start.3
  26.7 16.2 %collective-permute-start.11 = (bf16[48,4096]{1,0:T(8,128)(2,1)S(1)}, bf16[48,4096]{1,0:T(8,128)(2,1)}, u32[]{:S(2)}, u32[]{:S(2)}) collective-permute-start(bf16[48,4096]{1,0:T(8,128)(2,1)S(1)} %collective-permute-done.4.refs_2_), channel_id=1, source_target_pairs={{0,2},{1,17},{2,0},{3,19},{4,6},{5,21},{6,4},{7,23},{8,10},{9,25},... | collective-permute-start | bytes 1179656 | tf_op jit(solution)/shard_map/ppermute | solution.py:184
  28.2 0.8 copy-start.7
  29.0 13.9 %collective-permute-start.10 = (bf16[48,4096]{1,0:T(8,128)(2,1)S(1)}, bf16[48,4096]{1,0:T(8,128)(2,1)}, u32[]{:S(2)}, u32[]{:S(2)}) collective-permute-start(bf16[48,4096]{1,0:T(8,128)(2,1)S(1)} %collective-permute-done.9.refs_4_), channel_id=1, source_target_pairs={{0,16},{1,3},{2,18},{3,1},{4,20},{5,7},{6,22},{7,5},{8,24},{9,11},... | collective-permute-start | bytes 1179656 | tf_op jit(solution)/shard_map/ppermute | solution.py:184
  30.5 15.1 %collective-permute-start.2 = (bf16[48,4096]{1,0:T(8,128)(2,1)}, bf16[48,4096]{1,0:T(8,128)(2,1)}, u32[]{:S(2)}, u32[]{:S(2)}) collective-permute-start(bf16[48,4096]{1,0:T(8,128)(2,1)} %collective-permute-done.1.refs_3_), channel_id=1, source_target_pairs={{0,4},{1,13},{2,6},{3,15},{4,8},{5,1},{6,10},{7,3},{8,12},{9,5},{1... | collective-permute-start | bytes 1179656 | tf_op jit(solution)/shard_map/ppermute | solution.py:184
  38.6 4.3 %copy-start.5 = (bf16[48,4096]{1,0:T(8,128)(2,1)}, bf16[48,4096]{1,0:T(8,128)(2,1)S(1)}, u32[]{:S(2)}) copy-start(bf16[48,4096]{1,0:T(8,128)(2,1)S(1)} %collective-permute-done.5.refs_3_) | copy-start | bytes 1179652
  38.6 21.4 %collective-permute-start.12 = (bf16[48,4096]{1,0:T(8,128)(2,1)S(1)}, bf16[48,4096]{1,0:T(8,128)(2,1)}, u32[]{:S(2)}, u32[]{:S(2)}) collective-permute-start(bf16[48,4096]{1,0:T(8,128)(2,1)S(1)} %collective-permute-done.9.refs_4_), channel_id=1, source_target_pairs={{0,2},{1,17},{2,0},{3,19},{4,6},{5,21},{6,4},{7,23},{8,10},{9,25},... | collective-permute-start | bytes 1179656 | tf_op jit(solution)/shard_map/ppermute | solution.py:184
  42.8 17.1 %collective-permute-start.13 = (bf16[48,4096]{1,0:T(8,128)(2,1)}, bf16[48,4096]{1,0:T(8,128)(2,1)}, u32[]{:S(2)}, u32[]{:S(2)}) collective-permute-start(bf16[48,4096]{1,0:T(8,128)(2,1)} %collective-permute-done.11.refs_2_), channel_id=1, source_target_pairs={{0,16},{1,3},{2,18},{3,1},{4,20},{5,7},{6,22},{7,5},{8,24},{9,11},... | collective-permute-start | bytes 1179656 | tf_op jit(solution)/shard_map/ppermute | solution.py:184
  42.9 21.1 %collective-permute-start.6 = (bf16[48,4096]{1,0:T(8,128)(2,1)}, bf16[48,4096]{1,0:T(8,128)(2,1)}, u32[]{:S(2)}, u32[]{:S(2)}) collective-permute-start(bf16[48,4096]{1,0:T(8,128)(2,1)} %copy-done.5), channel_id=1, source_target_pairs={{0,2},{1,17},{2,0},{3,19},{4,6},{5,21},{6,4},{7,23},{8,10},{9,25},... | collective-permute-start | bytes 1179656 | tf_op jit(solution)/shard_map/ppermute | solution.py:184
  45.6 18.4 %collective-permute-start.7 = (bf16[48,4096]{1,0:T(8,128)(2,1)}, bf16[48,4096]{1,0:T(8,128)(2,1)}, u32[]{:S(2)}, u32[]{:S(2)}) collective-permute-start(bf16[48,4096]{1,0:T(8,128)(2,1)} %copy-done.5), channel_id=1, source_target_pairs={{0,16},{1,3},{2,18},{3,1},{4,20},{5,7},{6,22},{7,5},{8,24},{9,11},... | collective-permute-start | bytes 1179656 | tf_op jit(solution)/shard_map/ppermute | solution.py:184
  46.0 18.1 %collective-permute-start.3 = (bf16[48,4096]{1,0:T(8,128)(2,1)}, bf16[48,4096]{1,0:T(8,128)(2,1)}, u32[]{:S(2)}, u32[]{:S(2)}) collective-permute-start(bf16[48,4096]{1,0:T(8,128)(2,1)} %collective-permute-done.2.refs_0_), channel_id=1, source_target_pairs={{0,4},{1,13},{2,6},{3,15},{4,8},{5,1},{6,10},{7,3},{8,12},{9,5},{1... | collective-permute-start | bytes 1179656 | tf_op jit(solution)/shard_map/ppermute | solution.py:184
  51.7 1.6 %copy-start = (bf16[256,4096]{1,0:T(8,128)(2,1)S(1)}, bf16[256,4096]{1,0:T(8,128)(2,1)}, u32[]{:S(2)}) copy-start(bf16[256,4096]{1,0:T(8,128)(2,1)} %refs_3_.1) | copy-start | bytes 6291460
  53.3 1.0 %copy-start.2 = (bf16[48,4096]{1,0:T(8,128)(2,1)S(1)}, bf16[48,4096]{1,0:T(8,128)(2,1)}, u32[]{:S(2)}) copy-start(bf16[48,4096]{1,0:T(8,128)(2,1)} %refs_0_.1) | copy-start | bytes 1179652
  54.3 1.0 %copy-start.4 = (bf16[48,4096]{1,0:T(8,128)(2,1)S(1)}, bf16[48,4096]{1,0:T(8,128)(2,1)}, u32[]{:S(2)}) copy-start(bf16[48,4096]{1,0:T(8,128)(2,1)} %copy-done.3) | copy-start | bytes 1179652
  55.3 1.0 %copy-start.8 = (bf16[48,4096]{1,0:T(8,128)(2,1)S(1)}, bf16[48,4096]{1,0:T(8,128)(2,1)}, u32[]{:S(2)}) copy-start(bf16[48,4096]{1,0:T(8,128)(2,1)} %copy-done.7) | copy-start | bytes 1179652
  56.3 3.7 %copy-start.1 = (bf16[256,4096]{1,0:T(8,128)(2,1)S(1)}, bf16[256,4096]{1,0:T(8,128)(2,1)}, u32[]{:S(2)}) copy-start(bf16[256,4096]{1,0:T(8,128)(2,1)} %refs_3_.1) | copy-start | bytes 6291460
  56.3 3.7 %copy-start.6 = (bf16[48,4096]{1,0:T(8,128)(2,1)S(1)}, bf16[48,4096]{1,0:T(8,128)(2,1)}, u32[]{:S(2)}) copy-start(bf16[48,4096]{1,0:T(8,128)(2,1)} %copy-done.5) | copy-start | bytes 1179652
  66.7 5.6 %collective-permute-start.16 = (f32[32,48]{1,0:T(8,128)S(1)}, f32[32,48]{1,0:T(8,128)S(1)}, u32[]{:S(2)}, u32[]{:S(2)}) collective-permute-start(f32[32,48]{1,0:T(8,128)S(1)} %score.5), channel_id=1, source_target_pairs={{0,4},{1,5},{2,6},{3,7},{4,8},{5,9},{6,10},{7,11},{8,12},{9,13},{1... | collective-permute-start | bytes 18440 | tf_op jit(solution)/shard_map/ppermute | solution.py:184
  66.8 5.6 %collective-permute-start.17 = (f32[32,48]{1,0:T(8,128)S(1)}, f32[32,48]{1,0:T(8,128)S(1)}, u32[]{:S(2)}, u32[]{:S(2)}) collective-permute-start(f32[32,48]{1,0:T(8,128)S(1)} %score.5), channel_id=1, source_target_pairs={{0,8},{1,9},{2,10},{3,11},{4,12},{5,13},{6,14},{7,15},{8,0},{9,1},... | collective-permute-start | bytes 18440 | tf_op jit(solution)/shard_map/ppermute | solution.py:184
  67.0 5.9 %collective-permute-start.18 = (f32[32,48]{1,0:T(8,128)S(1)}, f32[32,48]{1,0:T(8,128)S(1)}, u32[]{:S(2)}, u32[]{:S(2)}) collective-permute-start(f32[32,48]{1,0:T(8,128)S(1)} %score.5), channel_id=1, source_target_pairs={{0,12},{1,13},{2,14},{3,15},{4,0},{5,1},{6,2},{7,3},{8,4},{9,5},{1... | collective-permute-start | bytes 18440 | tf_op jit(solution)/shard_map/ppermute | solution.py:184
  72.9 3.8 %collective-permute-start.19 = (f32[32,48]{1,0:T(8,128)S(1)}, f32[32,48]{1,0:T(8,128)S(1)}, u32[]{:S(2)}, u32[]{:S(2)}) collective-permute-start(f32[32,48]{1,0:T(8,128)S(1)} %pad_maximum_fusion), channel_id=1, source_target_pairs={{0,2},{1,3},{2,0},{3,1},{4,6},{5,7},{6,4},{7,5},{8,10},{9,11},{10,... | collective-permute-start | bytes 18440 | tf_op jit(solution)/shard_map/ppermute | solution.py:184
  73.2 3.7 %collective-permute-start.20 = (f32[32,48]{1,0:T(8,128)S(1)}, f32[32,48]{1,0:T(8,128)S(1)}, u32[]{:S(2)}, u32[]{:S(2)}) collective-permute-start(f32[32,48]{1,0:T(8,128)S(1)} %pad_maximum_fusion), channel_id=1, source_target_pairs={{0,16},{1,17},{2,18},{3,19},{4,20},{5,21},{6,22},{7,23},{8,24},{9,... | collective-permute-start | bytes 18440 | tf_op jit(solution)/shard_map/ppermute | solution.py:184
  73.9 4.6 %collective-permute-start.21 = (f32[32,48]{1,0:T(8,128)S(1)}, f32[32,48]{1,0:T(8,128)S(1)}, u32[]{:S(2)}, u32[]{:S(2)}) collective-permute-start(f32[32,48]{1,0:T(8,128)S(1)} %pad_maximum_fusion), channel_id=1, source_target_pairs={{0,18},{1,19},{2,16},{3,17},{4,22},{5,23},{6,20},{7,21},{8,26},{9,... | collective-permute-start | bytes 18440 | tf_op jit(solution)/shard_map/ppermute | solution.py:184
  79.2 1.2 %collective-permute-start.22 = (f32[16,48]{1,0:T(8,128)S(1)}, f32[16,48]{1,0:T(8,128)S(1)}, u32[]{:S(2)}, u32[]{:S(2)}) collective-permute-start(f32[16,48]{1,0:T(8,128)S(1)} %get-tuple-element.3), channel_id=1, source_target_pairs={{0,1},{1,0},{2,3},{3,2},{4,5},{5,4},{6,7},{7,6},{8,9},{9,8},{10,11... | collective-permute-start | bytes 9224 | tf_op jit(solution)/shard_map/ppermute | solution.py:184
where the time goes:
time: 83.8 us; the launch traced here: 83.4 us
  starting transfers between devices  40.8 us (49%)
  waiting for transfers between devices  19.6 us (23%)
  Pallas kernels  10.4 us (12%)
  local copies, waits for them, and re-layouts  7.37 us (9%)
  between operations  3.14 us (4%)
  other arithmetic  2.05 us (2%)
    ppermute x23, starting transfers between devices, moved(): return lax.ppermute(array, AXES, pairs)  40.8 us
    ppermute x23, waiting for transfers between devices, moved(): return lax.ppermute(array, AXES, pairs)  19.6 us
    pallas_call x3, Pallas kernels, score(): pl.pallas_call(functools.partial(score_kernel, count, slots), out_shape=j...  10.4 us
    unnamed x18, local copies, waits for them, and re-layouts  6.09 us
  transfers between devices with their start and end apart: 23, of which 10 were waited for; matrix products, arithmetic and copies ran while one was open for 2% of the time, Pallas kernels for 9%

commit v1 on v0

--- a/solution.py
+++ b/solution.py
@@ -11,22 +11,22 @@
 
 
 AXES = ("dp", "ring", "core")
-SEED = 6000647
-
-
-def plus(at, step, dims):
-    return tuple((a + s) % n for a, s, n in zip(at, step, dims))
-
-
-def minus(at, step, dims):
-    return tuple((a - s) % n for a, s, n in zip(at, step, dims))
+SEED = 2000322
+PIECES = 4
+VMEM_MIB = 24
+
+
+def across(at, step):
+    return tuple(a ^ s for a, s in zip(at, step))
 
 
 def hops_of(dims):
     out = []
     for k, n in enumerate(dims):
-        for way in sorted({1 % n, -1 % n} - {0}):
+        way = 1
+        while way < n:
             out.append((k, tuple(way if i == k else 0 for i in range(len(dims)))))
+            way = 2 * way + 1
     return out
 
 
@@ -49,11 +49,11 @@
         options = []
         for source in range(max(1, k - lag + 1)):
             for even in hops:
-                to_even = plus(places[0][source], even[1], dims)
+                to_even = across(places[0][source], even[1])
                 if used[0][even[0]] >= cap or to_even in places[0]:
                     continue
                 for odd in hops:
-                    to_odd = plus(places[1][source], odd[1], dims)
+                    to_odd = across(places[1][source], odd[1])
                     if apart and odd[0] == even[0]:
                         continue
                     if used[1][odd[0]] >= cap or to_odd in places[1]:
@@ -135,25 +135,53 @@
             bytes_accessed=2 * width * (rows + tok * count),
             transcendentals=rows * tok * count,
         ),
-        compiler_params=pltpu.CompilerParams(vmem_limit_bytes=24 * 1024 * 1024),
+        compiler_params=pltpu.CompilerParams(vmem_limit_bytes=VMEM_MIB * 2**20),
         name="score",
     )(slot_of, dev_of, bases, *blocks, mine, theirs, targets, kept)
 
 
 def batches_of(dims):
     total = math.prod(dims)
-    last = total - len(dims)
-    edges = (0, (last + 1) // 2, last, total)
+    early = total - len(dims)
+    edges = [early * i // PIECES for i in range(PIECES + 1)] + [total]
     return [tuple(range(low, high)) for low, high in zip(edges[:-1], edges[1:])]
+
+
+def tree(op, parts):
+    while len(parts) > 1:
+        parts = [op(*parts[i : i + 2]) if i + 1 < len(parts) else parts[i] for i in range(0, len(parts), 2)]
+    return parts[0]
 
 
 def joined(parts):
     half = parts[0].shape[0] // 2
     levels = [p[:half] for p in parts]
-    top = functools.reduce(jnp.maximum, levels)
-    total = functools.reduce(jnp.add, [jnp.exp(x - top) for x in levels])
-    picked = functools.reduce(jnp.add, [p[half:] for p in parts])
-    return jnp.concatenate([top + jnp.log(total), picked], axis=0)
+    top = tree(jnp.maximum, levels)
+    total = tree(jnp.add, [jnp.exp(x - top) for x in levels])
+    return top + jnp.log(total), tree(jnp.add, [p[half:] for p in parts])
+
+
+def finish_kernel(row_ref, mine, theirs, token_loss, mean_loss):
+    token_loss[...] = mine[pl.ds(row_ref[0], 1), :]
+    count = mine.shape[0] * mine.shape[1] * 2
+    total = jnp.sum(mine[...], keepdims=True) + jnp.sum(theirs[...], keepdims=True)
+    mean_loss[...] = total / count
+
+
+def finish(row, mine, theirs):
+    vmem = pl.BlockSpec(memory_space=pltpu.VMEM)
+    token_loss, mean_loss = pl.pallas_call(
+        finish_kernel,
+        out_shape=(
+            jax.ShapeDtypeStruct((1, mine.shape[1]), jnp.float32),
+            jax.ShapeDtypeStruct((1, 1), jnp.float32),
+        ),
+        in_specs=[pl.BlockSpec(memory_space=pltpu.SMEM), vmem, vmem],
+        out_specs=(vmem, vmem),
+        compiler_params=pltpu.CompilerParams(vmem_limit_bytes=VMEM_MIB * 2**20),
+        name="finish",
+    )(row.reshape(1), mine, theirs)
+    return token_loss.reshape(mine.shape[1]), mean_loss.reshape(())
 
 
 def local(mesh_sizes, dims, hidden, embedding, targets):
@@ -179,7 +207,7 @@
         pairs = []
         for i, spot in enumerate(spots):
             for c in range(cores):
-                to = index[plus(spot, steps[c], dims)]
+                to = index[across(spot, steps[c])]
                 pairs.append((i * cores + c, to * cores + (cores - 1 - c if swap else c)))
         return lax.ppermute(array, AXES, pairs)
 
@@ -188,7 +216,7 @@
     theirs = moved(embedding, still, swap=True)
 
     owners = jnp.array(
-        [[[index[minus(spot, at, dims)] for at in places[c]] for c in range(cores)] for spot in spots],
+        [[[index[across(spot, at)] for at in places[c]] for c in range(cores)] for spot in spots],
         jnp.int32,
     )
     slot_of = owners[chip, core]
@@ -206,16 +234,16 @@
             slots, [blocks[s] for s in slots], embedding, theirs, wanted, stats, slot_of, dev_of, bases
         )
 
-    turns = [plus(still[0], s, dims) for s in spots[1:]]
-    along = [t for t in turns if sum(1 for v in t if v) == 1 and t[1]]
-    across = [t for t in turns if not t[1]]
-    stats = joined([stats] + [moved(stats, (t,) * cores) for t in along])
-    stats = joined([stats] + [moved(stats, (t,) * cores) for t in across])
-    losses = stats[:chips] - stats[chips:]
-    other = moved(losses, still, swap=True)
-    mean_loss = (jnp.sum(losses) + jnp.sum(other)) / (tok * chips * cores)
-    token_loss = lax.dynamic_slice_in_dim(losses, chip, 1).reshape(tok)
-    return token_loss, mean_loss
+    long = dims.index(max(dims))
+    turns = [
+        [t for t in spots[1:] if not any(v for k, v in enumerate(t) if k != long)],
+        [t for t in spots[1:] if not t[long]],
+    ]
+    for stage in turns:
+        level, picked = joined([stats] + [moved(stats, (t,) * cores) for t in stage])
+        stats = jnp.concatenate([level, picked], axis=0)
+    losses = level - picked
+    return finish(chip, losses, moved(losses, still, swap=True))
 
 
 def gathered(hidden, embedding, targets):

time: 83.8 us -> 87.2 us (1.041)
  starting transfers between devices: 40.8 us -> 53.7 us
  waiting for transfers between devices: 19.6 us -> 14 us
  local copies, waits for them, and re-layouts: 7.37 us -> 4.12 us
  Pallas kernels: 10.4 us -> 13.4 us
  between operations: 3.14 us -> 0.74 us
  other arithmetic: 2.05 us -> 0.82 us
    ppermute x23, starting transfers between devices: 40.8 us -> 53.7 us  [moved(): return lax.ppermute(array, AXES, pairs)]
    ppermute x23, waiting for transfers between devices: 19.6 us -> 14 us  [moved(): return lax.ppermute(array, AXES, pairs)]
    unnamed x18 -> x10, local copies, waits for them, and re-layouts: 6.09 us -> 3.35 us
    pallas_call x3 -> x5, Pallas kernels: 10.4 us -> 12.7 us  [score(): pl.pallas_call(functools.partial(score_kernel, count, slots), out_shape=j...]
    reduce_sum x2 -> x0, other arithmetic: 1.25 us -> none  [share(): mean_loss = (jnp.sum(losses) + jnp.sum(other)) / (tok * chips * cores)]
  transfers between devices with their start and end apart: 23 -> 23, of which waited for: 10 -> 9; matrix products, arithmetic and copies ran while one was open for 2% -> 2% of each run, Pallas kernels for 9% -> 12%
where the time goes in v1:
time: 87.2 us; the launch traced here: 86.8 us
  starting transfers between devices  53.7 us (62%)
  waiting for transfers between devices  14 us (16%)
  Pallas kernels  13.4 us (15%)
  local copies, waits for them, and re-layouts  4.12 us (5%)
    ppermute x23, starting transfers between devices, moved(): return lax.ppermute(array, AXES, pairs)  53.7 us
    ppermute x23, waiting for transfers between devices, moved(): return lax.ppermute(array, AXES, pairs)  14 us
    pallas_call x5, Pallas kernels, score(): pl.pallas_call(functools.partial(score_kernel, count, slots), out_shape=j...  12.7 us
    unnamed x10, local copies, waits for them, and re-layouts  3.35 us
  transfers between devices with their start and end apart: 23, of which 9 were waited for; matrix products, arithmetic and copies ran while one was open for 2% of the time, Pallas kernels for 12%

profile of v1, /device:TPU:0, one launch (start us, length us, event | category | flops | bytes accessed | tf_op | source)
XLA Modules:
  0.0 86.8 jit_solution(15460777283637914648)
XLA Ops:
  1.2 2.6 %collective-permute-start.2 = (bf16[48,4096]{1,0:T(8,128)(2,1)}, bf16[48,4096]{1,0:T(8,128)(2,1)S(1)}, u32[]{:S(2)}, u32[]{:S(2)}) collective-permute-start(bf16[48,4096]{1,0:T(8,128)(2,1)} %refs_0_.1), channel_id=1, source_target_pairs={{0,4},{1,13},{2,6},{3,15},{4,0},{5,9},{6,2},{7,11},{8,12},{9,5},{1... | collective-permute-start | bytes 1179656 | tf_op jit(solution)/shard_map/ppermute | solution.py:212
  3.8 1.5 %collective-permute-start.12 = (bf16[48,4096]{1,0:T(8,128)(2,1)}, bf16[48,4096]{1,0:T(8,128)(2,1)S(1)}, u32[]{:S(2)}, u32[]{:S(2)}) collective-permute-start(bf16[48,4096]{1,0:T(8,128)(2,1)} %refs_0_.1), channel_id=1, source_target_pairs={{0,16},{1,3},{2,18},{3,1},{4,20},{5,7},{6,22},{7,5},{8,24},{9,11},... | collective-permute-start | bytes 1179656 | tf_op jit(solution)/shard_map/ppermute | solution.py:212
  5.3 1.5 %collective-permute-start.9 = (bf16[48,4096]{1,0:T(8,128)(2,1)}, bf16[48,4096]{1,0:T(8,128)(2,1)}, u32[]{:S(2)}, u32[]{:S(2)}) collective-permute-start(bf16[48,4096]{1,0:T(8,128)(2,1)} %refs_0_.1), channel_id=1, source_target_pairs={{0,2},{1,17},{2,0},{3,19},{4,6},{5,21},{6,4},{7,23},{8,10},{9,25},... | collective-permute-start | bytes 1179656 | tf_op jit(solution)/shard_map/ppermute | solution.py:212
  6.8 2.5 %collective-permute-start = (bf16[48,4096]{1,0:T(8,128)(2,1)}, bf16[48,4096]{1,0:T(8,128)(2,1)S(1)}, u32[]{:S(2)}, u32[]{:S(2)}) collective-permute-start(bf16[48,4096]{1,0:T(8,128)(2,1)} %refs_0_.1), channel_id=1, source_target_pairs={{0,12},{1,5},{2,14},{3,7},{4,8},{5,1},{6,10},{7,3},{8,4},{9,13},{1... | collective-permute-start | bytes 1179656 | tf_op jit(solution)/shard_map/ppermute | solution.py:212
  9.3 5.3 %collective-permute-done.2.refs_1_ = bf16[48,4096]{1,0:T(8,128)(2,1)S(1)} collective-permute-done((bf16[48,4096]{1,0:T(8,128)(2,1)}, bf16[48,4096]{1,0:T(8,128)(2,1)S(1)}, u32[]{:S(2)}, u32[]{:S(2)}) %collective-permute-start.2) | collective-permute-done | bytes 393248 | tf_op jit(solution)/shard_map/ppermute | solution.py:212
  14.6 10.3 %collective-permute-start.5 = (bf16[48,4096]{1,0:T(8,128)(2,1)S(1)}, bf16[48,4096]{1,0:T(8,128)(2,1)}, u32[]{:S(2)}, u32[]{:S(2)}) collective-permute-start(bf16[48,4096]{1,0:T(8,128)(2,1)S(1)} %collective-permute-done.2.refs_1_), channel_id=1, source_target_pairs={{0,12},{1,5},{2,14},{3,7},{4,8},{5,1},{6,10},{7,3},{8,4},{9,13},{1... | collective-permute-start | bytes 1179656 | tf_op jit(solution)/shard_map/ppermute | solution.py:212
  24.9 2.2 %collective-permute-start.13 = (bf16[48,4096]{1,0:T(8,128)(2,1)S(1)}, bf16[48,4096]{1,0:T(8,128)(2,1)S(1)}, u32[]{:S(2)}, u32[]{:S(2)}) collective-permute-start(bf16[48,4096]{1,0:T(8,128)(2,1)S(1)} %collective-permute-done.12.refs_2_), channel_id=1, source_target_pairs={{0,2},{1,17},{2,0},{3,19},{4,6},{5,21},{6,4},{7,23},{8,10},{9,25},... | collective-permute-start | bytes 1179656 | tf_op jit(solution)/shard_map/ppermute | solution.py:212
  27.1 2.4 %collective-permute-start.3 = (bf16[48,4096]{1,0:T(8,128)(2,1)S(1)}, bf16[48,4096]{1,0:T(8,128)(2,1)}, u32[]{:S(2)}, u32[]{:S(2)}) collective-permute-start(bf16[48,4096]{1,0:T(8,128)(2,1)S(1)} %collective-permute-done.2.refs_1_), channel_id=1, source_target_pairs={{0,16},{1,3},{2,18},{3,1},{4,20},{5,7},{6,22},{7,5},{8,24},{9,11},... | collective-permute-start | bytes 1179656 | tf_op jit(solution)/shard_map/ppermute | solution.py:212
  29.6 3.3 %collective-permute-done.5.refs_1_ = bf16[48,4096]{1,0:T(8,128)(2,1)} collective-permute-done((bf16[48,4096]{1,0:T(8,128)(2,1)S(1)}, bf16[48,4096]{1,0:T(8,128)(2,1)}, u32[]{:S(2)}, u32[]{:S(2)}) %collective-permute-start.5) | collective-permute-done | bytes 393248 | tf_op jit(solution)/shard_map/ppermute | solution.py:212
  32.8 3.0 %collective-permute-start.10 = (bf16[48,4096]{1,0:T(8,128)(2,1)}, bf16[48,4096]{1,0:T(8,128)(2,1)}, u32[]{:S(2)}, u32[]{:S(2)}) collective-permute-start(bf16[48,4096]{1,0:T(8,128)(2,1)} %collective-permute-done.9.refs_0_), channel_id=1, source_target_pairs={{0,12},{1,5},{2,14},{3,7},{4,8},{5,1},{6,10},{7,3},{8,4},{9,13},{1... | collective-permute-start | bytes 1179656 | tf_op jit(solution)/shard_map/ppermute | solution.py:212
  35.9 0.8 copy-done.3
  36.6 2.6 %collective-permute-start.6 = (bf16[48,4096]{1,0:T(8,128)(2,1)}, bf16[48,4096]{1,0:T(8,128)(2,1)}, u32[]{:S(2)}, u32[]{:S(2)}) collective-permute-start(bf16[48,4096]{1,0:T(8,128)(2,1)} %collective-permute-done.5.refs_1_), channel_id=1, source_target_pairs={{0,2},{1,17},{2,0},{3,19},{4,6},{5,21},{6,4},{7,23},{8,10},{9,25},... | collective-permute-start | bytes 1179656 | tf_op jit(solution)/shard_map/ppermute | solution.py:212
  39.2 3.3 %collective-permute-start.1 = (bf16[48,4096]{1,0:T(8,128)(2,1)S(1)}, bf16[48,4096]{1,0:T(8,128)(2,1)}, u32[]{:S(2)}, u32[]{:S(2)}) collective-permute-start(bf16[48,4096]{1,0:T(8,128)(2,1)S(1)} %collective-permute-done.refs_0_), channel_id=1, source_target_pairs={{0,16},{1,3},{2,18},{3,1},{4,20},{5,7},{6,22},{7,5},{8,24},{9,11},... | collective-permute-start | bytes 1179656 | tf_op jit(solution)/shard_map/ppermute | solution.py:212
  42.6 2.7 %collective-permute-start.11 = (bf16[48,4096]{1,0:T(8,128)(2,1)}, bf16[48,4096]{1,0:T(8,128)(2,1)}, u32[]{:S(2)}, u32[]{:S(2)}) collective-permute-start(bf16[48,4096]{1,0:T(8,128)(2,1)} %collective-permute-done.5.refs_1_), channel_id=1, source_target_pairs={{0,16},{1,3},{2,18},{3,1},{4,20},{5,7},{6,22},{7,5},{8,24},{9,11},... | collective-permute-start | bytes 1179656 | tf_op jit(solution)/shard_map/ppermute | solution.py:212
  45.2 4.2 %collective-permute-start.14 = (bf16[48,4096]{1,0:T(8,128)(2,1)}, bf16[48,4096]{1,0:T(8,128)(2,1)}, u32[]{:S(2)}, u32[]{:S(2)}) collective-permute-start(bf16[48,4096]{1,0:T(8,128)(2,1)} %copy-done.3), channel_id=1, source_target_pairs={{0,12},{1,5},{2,14},{3,7},{4,8},{5,1},{6,10},{7,3},{8,4},{9,13},{1... | collective-permute-start | bytes 1179656 | tf_op jit(solution)/shard_map/ppermute | solution.py:212
  49.9 2.7 %collective-permute-start.4 = (bf16[48,4096]{1,0:T(8,128)(2,1)}, bf16[48,4096]{1,0:T(8,128)(2,1)}, u32[]{:S(2)}, u32[]{:S(2)}) collective-permute-start(bf16[48,4096]{1,0:T(8,128)(2,1)} %collective-permute-done.3.refs_2_), channel_id=1, source_target_pairs={{0,2},{1,17},{2,0},{3,19},{4,6},{5,21},{6,4},{7,23},{8,10},{9,25},... | collective-permute-start | bytes 1179656 | tf_op jit(solution)/shard_map/ppermute | solution.py:212
  52.6 3.6 %collective-permute-start.7 = (bf16[48,4096]{1,0:T(8,128)(2,1)}, bf16[48,4096]{1,0:T(8,128)(2,1)}, u32[]{:S(2)}, u32[]{:S(2)}) collective-permute-start(bf16[48,4096]{1,0:T(8,128)(2,1)} %collective-permute-done.6.refs_0_), channel_id=1, source_target_pairs={{0,16},{1,3},{2,18},{3,1},{4,20},{5,7},{6,22},{7,5},{8,24},{9,11},... | collective-permute-start | bytes 1179656 | tf_op jit(solution)/shard_map/ppermute | solution.py:212
  56.3 0.8 reshape.17.refs_5_.refs_6_
  57.1 0.7 multiply_add_fusion
  57.8 1.6 %copy-done = bf16[256,4096]{1,0:T(8,128)(2,1)S(1)} copy-done((bf16[256,4096]{1,0:T(8,128)(2,1)S(1)}, bf16[256,4096]{1,0:T(8,128)(2,1)}, u32[]{:S(2)}) %copy-start) | copy-done | bytes 2097176
  59.4 1.0 %copy-done.2 = bf16[48,4096]{1,0:T(8,128)(2,1)S(1)} copy-done((bf16[48,4096]{1,0:T(8,128)(2,1)S(1)}, bf16[48,4096]{1,0:T(8,128)(2,1)}, u32[]{:S(2)}) %copy-start.2) | copy-done | bytes 393240
  60.4 2.0 %score.5.refs_6_ = f32[32,48]{1,0:T(8,128)S(1)} custom-call(s32[16]{0:T(128)S(1)} %get-tuple-element.7.slot_ref, s32[16]{0:T(128)S(1)} %get-tuple-element.6.dev_ref, s32[2]{0:T(128)S(1)} %pad_add_fusion.base_ref, bf16[48,4096]{1,0:T(8,128)(2,1)S(1)} %copy-done.2, bf16[48,4096]{1,0:T(8,128)(2,1)S(1)} %collective-permute-done.2.refs_1_, ...), custom_call_target="tpu_custom_call" | custom-call | flops 603979776 | bytes 5373952 | tf_op jit(solution)/shard_map/score/pallas_call | solution.py:128
  62.4 2.6 %score.6.refs_6_ = f32[32,48]{1,0:T(8,128)S(1)} custom-call(s32[16]{0:T(128)S(1)} %get-tuple-element.7.slot_ref, s32[16]{0:T(128)S(1)} %get-tuple-element.6.dev_ref, s32[2]{0:T(128)S(1)} %pad_add_fusion.base_ref, bf16[48,4096]{1,0:T(8,128)(2,1)} %collective-permute-done.9.refs_0_, bf16[48,4096]{1,0:T(8,128)(2,1)} %collective-permute-done.5.refs_1_, ...), custom_call_target="tpu_custom_call" | custom-call | flops 603979776 | bytes 5373952 | tf_op jit(solution)/shard_map/score/pallas_call | solution.py:128
  65.0 2.6 %score.7.refs_7_ = f32[32,48]{1,0:T(8,128)S(1)} custom-call(s32[16]{0:T(128)S(1)} %get-tuple-element.7.slot_ref, s32[16]{0:T(128)S(1)} %get-tuple-element.6.dev_ref, s32[2]{0:T(128)S(1)} %pad_add_fusion.base_ref, bf16[48,4096]{1,0:T(8,128)(2,1)S(1)} %collective-permute-done.refs_0_, bf16[48,4096]{1,0:T(8,128)(2,1)} %collective-permute-done.15.refs_1_, ...), custom_call_target="tpu_custom_call" | custom-call | flops 603979776 | bytes 5373952 | tf_op jit(solution)/shard_map/score/pallas_call | solution.py:128
  67.6 2.8 %score.8.refs_6_ = f32[32,48]{1,0:T(8,128)S(1)} custom-call(s32[16]{0:T(128)S(1)} %get-tuple-element.7.slot_ref, s32[16]{0:T(128)S(1)} %get-tuple-element.6.dev_ref, s32[2]{0:T(128)S(1)} %pad_add_fusion.base_ref, bf16[48,4096]{1,0:T(8,128)(2,1)} %collective-permute-done.6.refs_0_, bf16[48,4096]{1,0:T(8,128)(2,1)} %collective-permute-done.10.refs_1_, ...), custom_call_target="tpu_custom_call" | custom-call | flops 805306368 | bytes 5767168 | tf_op jit(solution)/shard_map/score/pallas_call | solution.py:128
  70.4 2.7 %score.9 = f32[32,48]{1,0:T(8,128)S(1)} custom-call(s32[16]{0:T(128)S(1)} %get-tuple-element.7.slot_ref, s32[16]{0:T(128)S(1)} %get-tuple-element.6.dev_ref, s32[2]{0:T(128)S(1)} %pad_add_fusion.base_ref, bf16[48,4096]{1,0:T(8,128)(2,1)} %collective-permute-done.1.refs_0_, bf16[48,4096]{1,0:T(8,128)(2,1)} %collective-permute-done.4.refs_1_, ...), custom_call_target="tpu_custom_call" | custom-call | flops 603979776 | bytes 5373952 | tf_op jit(solution)/shard_map/score/pallas_call | solution.py:128
  73.2 4.3 %collective-permute-start.18 = (f32[32,48]{1,0:T(8,128)S(1)}, f32[32,48]{1,0:T(8,128)S(1)}, u32[]{:S(2)}, u32[]{:S(2)}) collective-permute-start(f32[32,48]{1,0:T(8,128)S(1)} %score.9), channel_id=1, source_target_pairs={{0,12},{1,13},{2,14},{3,15},{4,8},{5,9},{6,10},{7,11},{8,4},{9,5},... | collective-permute-start | bytes 18440 | tf_op jit(solution)/shard_map/ppermute | solution.py:212
  77.9 1.6 %collective-permute-done.18 = f32[32,48]{1,0:T(8,128)S(1)} collective-permute-done((f32[32,48]{1,0:T(8,128)S(1)}, f32[32,48]{1,0:T(8,128)S(1)}, u32[]{:S(2)}, u32[]{:S(2)}) %collective-permute-start.18) | collective-permute-done | bytes 6176 | tf_op jit(solution)/shard_map/ppermute | solution.py:212
  79.6 3.4 %collective-permute-start.21 = (f32[32,48]{1,0:T(8,128)S(1)}, f32[32,48]{1,0:T(8,128)S(1)}, u32[]{:S(2)}, u32[]{:S(2)}) collective-permute-start(f32[32,48]{1,0:T(8,128)S(1)} %pad_maximum_fusion), channel_id=1, source_target_pairs={{0,18},{1,19},{2,16},{3,17},{4,22},{5,23},{6,20},{7,21},{8,26},{9,... | collective-permute-start | bytes 18440 | tf_op jit(solution)/shard_map/ppermute | solution.py:212
  83.4 1.6 %collective-permute-done.21 = f32[32,48]{1,0:T(8,128)S(1)} collective-permute-done((f32[32,48]{1,0:T(8,128)S(1)}, f32[32,48]{1,0:T(8,128)S(1)}, u32[]{:S(2)}, u32[]{:S(2)}) %collective-permute-start.21) | collective-permute-done | bytes 6176 | tf_op jit(solution)/shard_map/ppermute | solution.py:212
  85.0 1.2 %collective-permute-done.22.theirs = f32[16,48]{1,0:T(8,128)S(1)} collective-permute-done((f32[16,48]{1,0:T(8,128)S(1)}, f32[16,48]{1,0:T(8,128)S(1)}, u32[]{:S(2)}, u32[]{:S(2)}) %collective-permute-start.22) | collective-permute-done | bytes 3104 | tf_op jit(solution)/shard_map/ppermute | solution.py:212
  86.2 0.6 finish.1
  (37 shorter events, 2.3 us)
Async XLA Ops:
  0.6 52.0 %collective-permute-start.8 = (bf16[256,4096]{1,0:T(8,128)(2,1)}, bf16[256,4096]{1,0:T(8,128)(2,1)S(1)}, u32[]{:S(2)}, u32[]{:S(2)}) collective-permute-start(bf16[256,4096]{1,0:T(8,128)(2,1)} %refs_3_.7), channel_id=1, source_target_pairs={{0,1},{1,0},{2,3},{3,2},{4,5},{5,4},{6,7},{7,6},{8,9},{9,8},{10,11... | collective-permute-start | bytes 6291464 | tf_op jit(solution)/shard_map/ppermute | solution.py:212
  1.2 13.4 %collective-permute-start.2 = (bf16[48,4096]{1,0:T(8,128)(2,1)}, bf16[48,4096]{1,0:T(8,128)(2,1)S(1)}, u32[]{:S(2)}, u32[]{:S(2)}) collective-permute-start(bf16[48,4096]{1,0:T(8,128)(2,1)} %refs_0_.1), channel_id=1, source_target_pairs={{0,4},{1,13},{2,6},{3,15},{4,0},{5,9},{6,2},{7,11},{8,12},{9,5},{1... | collective-permute-start | bytes 1179656 | tf_op jit(solution)/shard_map/ppermute | solution.py:212
  3.8 21.1 %collective-permute-start.12 = (bf16[48,4096]{1,0:T(8,128)(2,1)}, bf16[48,4096]{1,0:T(8,128)(2,1)S(1)}, u32[]{:S(2)}, u32[]{:S(2)}) collective-permute-start(bf16[48,4096]{1,0:T(8,128)(2,1)} %refs_0_.1), channel_id=1, source_target_pairs={{0,16},{1,3},{2,18},{3,1},{4,20},{5,7},{6,22},{7,5},{8,24},{9,11},... | collective-permute-start | bytes 1179656 | tf_op jit(solution)/shard_map/ppermute | solution.py:212
  5.3 21.8 %collective-permute-start.9 = (bf16[48,4096]{1,0:T(8,128)(2,1)}, bf16[48,4096]{1,0:T(8,128)(2,1)}, u32[]{:S(2)}, u32[]{:S(2)}) collective-permute-start(bf16[48,4096]{1,0:T(8,128)(2,1)} %refs_0_.1), channel_id=1, source_target_pairs={{0,2},{1,17},{2,0},{3,19},{4,6},{5,21},{6,4},{7,23},{8,10},{9,25},... | collective-permute-start | bytes 1179656 | tf_op jit(solution)/shard_map/ppermute | solution.py:212
  6.8 22.7 %collective-permute-start = (bf16[48,4096]{1,0:T(8,128)(2,1)}, bf16[48,4096]{1,0:T(8,128)(2,1)S(1)}, u32[]{:S(2)}, u32[]{:S(2)}) collective-permute-start(bf16[48,4096]{1,0:T(8,128)(2,1)} %refs_0_.1), channel_id=1, source_target_pairs={{0,12},{1,5},{2,14},{3,7},{4,8},{5,1},{6,10},{7,3},{8,4},{9,13},{1... | collective-permute-start | bytes 1179656 | tf_op jit(solution)/shard_map/ppermute | solution.py:212
  14.6 18.2 %collective-permute-start.5 = (bf16[48,4096]{1,0:T(8,128)(2,1)S(1)}, bf16[48,4096]{1,0:T(8,128)(2,1)}, u32[]{:S(2)}, u32[]{:S(2)}) collective-permute-start(bf16[48,4096]{1,0:T(8,128)(2,1)S(1)} %collective-permute-done.2.refs_1_), channel_id=1, source_target_pairs={{0,12},{1,5},{2,14},{3,7},{4,8},{5,1},{6,10},{7,3},{8,4},{9,13},{1... | collective-permute-start | bytes 1179656 | tf_op jit(solution)/shard_map/ppermute | solution.py:212
  24.9 11.0 %collective-permute-start.13 = (bf16[48,4096]{1,0:T(8,128)(2,1)S(1)}, bf16[48,4096]{1,0:T(8,128)(2,1)S(1)}, u32[]{:S(2)}, u32[]{:S(2)}) collective-permute-start(bf16[48,4096]{1,0:T(8,128)(2,1)S(1)} %collective-permute-done.12.refs_2_), channel_id=1, source_target_pairs={{0,2},{1,17},{2,0},{3,19},{4,6},{5,21},{6,4},{7,23},{8,10},{9,25},... | collective-permute-start | bytes 1179656 | tf_op jit(solution)/shard_map/ppermute | solution.py:212
  27.1 12.1 %collective-permute-start.3 = (bf16[48,4096]{1,0:T(8,128)(2,1)S(1)}, bf16[48,4096]{1,0:T(8,128)(2,1)}, u32[]{:S(2)}, u32[]{:S(2)}) collective-permute-start(bf16[48,4096]{1,0:T(8,128)(2,1)S(1)} %collective-permute-done.2.refs_1_), channel_id=1, source_target_pairs={{0,16},{1,3},{2,18},{3,1},{4,20},{5,7},{6,22},{7,5},{8,24},{9,11},... | collective-permute-start | bytes 1179656 | tf_op jit(solution)/shard_map/ppermute | solution.py:212
  29.5 13.0 %collective-permute-start.15 = (bf16[48,4096]{1,0:T(8,128)(2,1)S(1)}, bf16[48,4096]{1,0:T(8,128)(2,1)}, u32[]{:S(2)}, u32[]{:S(2)}) collective-permute-start(bf16[48,4096]{1,0:T(8,128)(2,1)S(1)} %collective-permute-done.2.refs_1_), channel_id=1, source_target_pairs={{0,2},{1,17},{2,0},{3,19},{4,6},{5,21},{6,4},{7,23},{8,10},{9,25},... | collective-permute-start | bytes 1179656 | tf_op jit(solution)/shard_map/ppermute | solution.py:212
  32.8 12.4 %collective-permute-start.10 = (bf16[48,4096]{1,0:T(8,128)(2,1)}, bf16[48,4096]{1,0:T(8,128)(2,1)}, u32[]{:S(2)}, u32[]{:S(2)}) collective-permute-start(bf16[48,4096]{1,0:T(8,128)(2,1)} %collective-permute-done.9.refs_0_), channel_id=1, source_target_pairs={{0,12},{1,5},{2,14},{3,7},{4,8},{5,1},{6,10},{7,3},{8,4},{9,13},{1... | collective-permute-start | bytes 1179656 | tf_op jit(solution)/shard_map/ppermute | solution.py:212
  35.9 0.8 copy-start.3
  36.6 13.2 %collective-permute-start.6 = (bf16[48,4096]{1,0:T(8,128)(2,1)}, bf16[48,4096]{1,0:T(8,128)(2,1)}, u32[]{:S(2)}, u32[]{:S(2)}) collective-permute-start(bf16[48,4096]{1,0:T(8,128)(2,1)} %collective-permute-done.5.refs_1_), channel_id=1, source_target_pairs={{0,2},{1,17},{2,0},{3,19},{4,6},{5,21},{6,4},{7,23},{8,10},{9,25},... | collective-permute-start | bytes 1179656 | tf_op jit(solution)/shard_map/ppermute | solution.py:212
  39.2 31.2 %collective-permute-start.1 = (bf16[48,4096]{1,0:T(8,128)(2,1)S(1)}, bf16[48,4096]{1,0:T(8,128)(2,1)}, u32[]{:S(2)}, u32[]{:S(2)}) collective-permute-start(bf16[48,4096]{1,0:T(8,128)(2,1)S(1)} %collective-permute-done.refs_0_), channel_id=1, source_target_pairs={{0,16},{1,3},{2,18},{3,1},{4,20},{5,7},{6,22},{7,5},{8,24},{9,11},... | collective-permute-start | bytes 1179656 | tf_op jit(solution)/shard_map/ppermute | solution.py:212
  42.6 25.0 %collective-permute-start.11 = (bf16[48,4096]{1,0:T(8,128)(2,1)}, bf16[48,4096]{1,0:T(8,128)(2,1)}, u32[]{:S(2)}, u32[]{:S(2)}) collective-permute-start(bf16[48,4096]{1,0:T(8,128)(2,1)} %collective-permute-done.5.refs_1_), channel_id=1, source_target_pairs={{0,16},{1,3},{2,18},{3,1},{4,20},{5,7},{6,22},{7,5},{8,24},{9,11},... | collective-permute-start | bytes 1179656 | tf_op jit(solution)/shard_map/ppermute | solution.py:212
  45.2 22.4 %collective-permute-start.14 = (bf16[48,4096]{1,0:T(8,128)(2,1)}, bf16[48,4096]{1,0:T(8,128)(2,1)}, u32[]{:S(2)}, u32[]{:S(2)}) collective-permute-start(bf16[48,4096]{1,0:T(8,128)(2,1)} %copy-done.3), channel_id=1, source_target_pairs={{0,12},{1,5},{2,14},{3,7},{4,8},{5,1},{6,10},{7,3},{8,4},{9,13},{1... | collective-permute-start | bytes 1179656 | tf_op jit(solution)/shard_map/ppermute | solution.py:212
  49.9 20.6 %collective-permute-start.4 = (bf16[48,4096]{1,0:T(8,128)(2,1)}, bf16[48,4096]{1,0:T(8,128)(2,1)}, u32[]{:S(2)}, u32[]{:S(2)}) collective-permute-start(bf16[48,4096]{1,0:T(8,128)(2,1)} %collective-permute-done.3.refs_2_), channel_id=1, source_target_pairs={{0,2},{1,17},{2,0},{3,19},{4,6},{5,21},{6,4},{7,23},{8,10},{9,25},... | collective-permute-start | bytes 1179656 | tf_op jit(solution)/shard_map/ppermute | solution.py:212
  52.6 17.8 %collective-permute-start.7 = (bf16[48,4096]{1,0:T(8,128)(2,1)}, bf16[48,4096]{1,0:T(8,128)(2,1)}, u32[]{:S(2)}, u32[]{:S(2)}) collective-permute-start(bf16[48,4096]{1,0:T(8,128)(2,1)} %collective-permute-done.6.refs_0_), channel_id=1, source_target_pairs={{0,16},{1,3},{2,18},{3,1},{4,20},{5,7},{6,22},{7,5},{8,24},{9,11},... | collective-permute-start | bytes 1179656 | tf_op jit(solution)/shard_map/ppermute | solution.py:212
  57.8 1.6 %copy-start = (bf16[256,4096]{1,0:T(8,128)(2,1)S(1)}, bf16[256,4096]{1,0:T(8,128)(2,1)}, u32[]{:S(2)}) copy-start(bf16[256,4096]{1,0:T(8,128)(2,1)} %refs_3_.7) | copy-start | bytes 6291460
  59.4 1.0 %copy-start.2 = (bf16[48,4096]{1,0:T(8,128)(2,1)S(1)}, bf16[48,4096]{1,0:T(8,128)(2,1)}, u32[]{:S(2)}) copy-start(bf16[48,4096]{1,0:T(8,128)(2,1)} %refs_0_.1) | copy-start | bytes 1179652
  60.4 2.0 %copy-start.1 = (bf16[256,4096]{1,0:T(8,128)(2,1)S(1)}, bf16[256,4096]{1,0:T(8,128)(2,1)}, u32[]{:S(2)}) copy-start(bf16[256,4096]{1,0:T(8,128)(2,1)} %refs_3_.7) | copy-start | bytes 6291460
  60.4 2.0 %copy-start.4 = (bf16[48,4096]{1,0:T(8,128)(2,1)S(1)}, bf16[48,4096]{1,0:T(8,128)(2,1)}, u32[]{:S(2)}) copy-start(bf16[48,4096]{1,0:T(8,128)(2,1)} %copy-done.3) | copy-start | bytes 1179652
  73.1 4.4 %collective-permute-start.16 = (f32[32,48]{1,0:T(8,128)S(1)}, f32[32,48]{1,0:T(8,128)S(1)}, u32[]{:S(2)}, u32[]{:S(2)}) collective-permute-start(f32[32,48]{1,0:T(8,128)S(1)} %score.9), channel_id=1, source_target_pairs={{0,4},{1,5},{2,6},{3,7},{4,0},{5,1},{6,2},{7,3},{8,12},{9,13},{10,... | collective-permute-start | bytes 18440 | tf_op jit(solution)/shard_map/ppermute | solution.py:212
  73.2 4.7 %collective-permute-start.17 = (f32[32,48]{1,0:T(8,128)S(1)}, f32[32,48]{1,0:T(8,128)S(1)}, u32[]{:S(2)}, u32[]{:S(2)}) collective-permute-start(f32[32,48]{1,0:T(8,128)S(1)} %score.9), channel_id=1, source_target_pairs={{0,8},{1,9},{2,10},{3,11},{4,12},{5,13},{6,14},{7,15},{8,0},{9,1},... | collective-permute-start | bytes 18440 | tf_op jit(solution)/shard_map/ppermute | solution.py:212
  73.2 6.2 %collective-permute-start.18 = (f32[32,48]{1,0:T(8,128)S(1)}, f32[32,48]{1,0:T(8,128)S(1)}, u32[]{:S(2)}, u32[]{:S(2)}) collective-permute-start(f32[32,48]{1,0:T(8,128)S(1)} %score.9), channel_id=1, source_target_pairs={{0,12},{1,13},{2,14},{3,15},{4,8},{5,9},{6,10},{7,11},{8,4},{9,5},... | collective-permute-start | bytes 18440 | tf_op jit(solution)/shard_map/ppermute | solution.py:212
  79.5 3.8 %collective-permute-start.19 = (f32[32,48]{1,0:T(8,128)S(1)}, f32[32,48]{1,0:T(8,128)S(1)}, u32[]{:S(2)}, u32[]{:S(2)}) collective-permute-start(f32[32,48]{1,0:T(8,128)S(1)} %pad_maximum_fusion), channel_id=1, source_target_pairs={{0,2},{1,3},{2,0},{3,1},{4,6},{5,7},{6,4},{7,5},{8,10},{9,11},{10,... | collective-permute-start | bytes 18440 | tf_op jit(solution)/shard_map/ppermute | solution.py:212
  79.5 3.8 %collective-permute-start.20 = (f32[32,48]{1,0:T(8,128)S(1)}, f32[32,48]{1,0:T(8,128)S(1)}, u32[]{:S(2)}, u32[]{:S(2)}) collective-permute-start(f32[32,48]{1,0:T(8,128)S(1)} %pad_maximum_fusion), channel_id=1, source_target_pairs={{0,16},{1,17},{2,18},{3,19},{4,20},{5,21},{6,22},{7,23},{8,24},{9,... | collective-permute-start | bytes 18440 | tf_op jit(solution)/shard_map/ppermute | solution.py:212
  79.6 5.3 %collective-permute-start.21 = (f32[32,48]{1,0:T(8,128)S(1)}, f32[32,48]{1,0:T(8,128)S(1)}, u32[]{:S(2)}, u32[]{:S(2)}) collective-permute-start(f32[32,48]{1,0:T(8,128)S(1)} %pad_maximum_fusion), channel_id=1, source_target_pairs={{0,18},{1,19},{2,16},{3,17},{4,22},{5,23},{6,20},{7,21},{8,26},{9,... | collective-permute-start | bytes 18440 | tf_op jit(solution)/shard_map/ppermute | solution.py:212
  84.9 1.2 %collective-permute-start.22 = (f32[16,48]{1,0:T(8,128)S(1)}, f32[16,48]{1,0:T(8,128)S(1)}, u32[]{:S(2)}, u32[]{:S(2)}) collective-permute-start(f32[16,48]{1,0:T(8,128)S(1)} %fusion.1.mine), channel_id=1, source_target_pairs={{0,1},{1,0},{2,3},{3,2},{4,5},{5,4},{6,7},{7,6},{8,9},{9,8},{10,11... | collective-permute-start | bytes 9224 | tf_op jit(solution)/shard_map/ppermute | solution.py:212

commit v2 on v1

--- a/solution.py
+++ b/solution.py
@@ -1,4 +1,5 @@
 import functools
+import itertools
 import math
 import random
 
@@ -11,7 +12,7 @@
 
 
 AXES = ("dp", "ring", "core")
-SEED = 2000322
+ORDER = ((0, 3, 1), (0, 4, 0), (0, 0, 4), (1, 1, 3), (1, 4, 0), (1, 0, 4), (3, 4, 0), (2, 1, 3), (4, 4, 0), (4, 0, 4), (3, 1, 3), (8, 4, 0), (6, 4, 0), (7, 1, 3), (9, 0, 4))
 PIECES = 4
 VMEM_MIB = 24
 
@@ -23,10 +24,8 @@
 def hops_of(dims):
     out = []
     for k, n in enumerate(dims):
-        way = 1
-        while way < n:
+        for way in range(1, n):
             out.append((k, tuple(way if i == k else 0 for i in range(len(dims)))))
-            way = 2 * way + 1
     return out
 
 
@@ -80,12 +79,26 @@
     return extend(1, [], (origin, origin), [[0] * len(dims)] * 2)
 
 
-def relay(dims, seed=SEED, tries=400):
-    while True:
-        found = attempt(dims, seed, tries)
-        if found:
-            return found
-        seed += 1
+def placed(dims, order):
+    hops = hops_of(dims)
+    steps, places = [], ([tuple(0 for _ in dims)], [tuple(0 for _ in dims)])
+    for source, even, odd in order:
+        if max(even, odd) >= len(hops):
+            return None
+        steps.append((source, hops[even], hops[odd]))
+        for core, (_, way) in enumerate(steps[-1][1:]):
+            places[core].append(across(places[core][source], way))
+    everywhere = set(itertools.product(*[range(n) for n in dims]))
+    if any(len(p) != len(everywhere) or set(p) != everywhere for p in places):
+        return None
+    return steps, places
+
+
+def relay(dims, tries=400):
+    found, seed = placed(dims, ORDER), 0
+    while not found:
+        found, seed = attempt(dims, seed, tries), seed + 1
+    return found
 
 
 def score_kernel(count, slots, slot_ref, dev_ref, base_ref, *refs):

time: 87.2 us -> 83.5 us (0.958)
  starting transfers between devices: 53.7 us -> 29.4 us
  waiting for transfers between devices: 14 us -> 34 us
    ppermute x23, starting transfers between devices: 53.7 us -> 29.4 us  [moved(): return lax.ppermute(array, AXES, pairs)]
    ppermute x23, waiting for transfers between devices: 14 us -> 34 us  [moved(): return lax.ppermute(array, AXES, pairs)]
    unnamed x10 -> x14, local copies, waits for them, and re-layouts: 3.35 us -> 4.1 us
  transfers between devices with their start and end apart: 23 -> 23, of which waited for: 9 -> 11; matrix products, arithmetic and copies ran while one was open for 2% -> 2% of each run, Pallas kernels for 12% -> 12%
where the time goes in v2:
time: 83.5 us; the launch traced here: 83.2 us
  waiting for transfers between devices  34 us (41%)
  starting transfers between devices  29.4 us (35%)
  Pallas kernels  13.3 us (16%)
  local copies, waits for them, and re-layouts  4.87 us (6%)
    ppermute x23, waiting for transfers between devices, moved(): return lax.ppermute(array, AXES, pairs)  34 us
    ppermute x23, starting transfers between devices, moved(): return lax.ppermute(array, AXES, pairs)  29.4 us
    pallas_call x5, Pallas kernels, score(): pl.pallas_call(functools.partial(score_kernel, count, slots), out_shape=j...  12.7 us
    unnamed x14, local copies, waits for them, and re-layouts  4.1 us
  transfers between devices with their start and end apart: 23, of which 11 were waited for; matrix products, arithmetic and copies ran while one was open for 2% of the time, Pallas kernels for 12%

profile of v2, /device:TPU:0, one launch (start us, length us, event | category | flops | bytes accessed | tf_op | source)
XLA Modules:
  0.0 83.2 jit_solution(1065182401686578064)
XLA Ops:
  1.2 4.7 %collective-permute-start = (bf16[48,4096]{1,0:T(8,128)(2,1)}, bf16[48,4096]{1,0:T(8,128)(2,1)S(1)}, u32[]{:S(2)}, u32[]{:S(2)}) collective-permute-start(bf16[48,4096]{1,0:T(8,128)(2,1)} %refs_0_.1), channel_id=1, source_target_pairs={{0,12},{1,5},{2,14},{3,7},{4,8},{5,1},{6,10},{7,3},{8,4},{9,13},{1... | collective-permute-start | bytes 1179656 | tf_op jit(solution)/shard_map/ppermute | solution.py:225
  5.9 1.5 %collective-permute-start.12 = (bf16[48,4096]{1,0:T(8,128)(2,1)}, bf16[48,4096]{1,0:T(8,128)(2,1)S(1)}, u32[]{:S(2)}, u32[]{:S(2)}) collective-permute-start(bf16[48,4096]{1,0:T(8,128)(2,1)} %refs_0_.1), channel_id=1, source_target_pairs={{0,2},{1,17},{2,0},{3,19},{4,6},{5,21},{6,4},{7,23},{8,10},{9,25},... | collective-permute-start | bytes 1179656 | tf_op jit(solution)/shard_map/ppermute | solution.py:225
  7.4 1.5 %collective-permute-start.3 = (bf16[48,4096]{1,0:T(8,128)(2,1)}, bf16[48,4096]{1,0:T(8,128)(2,1)S(1)}, u32[]{:S(2)}, u32[]{:S(2)}) collective-permute-start(bf16[48,4096]{1,0:T(8,128)(2,1)} %refs_0_.1), channel_id=1, source_target_pairs={{0,16},{1,3},{2,18},{3,1},{4,20},{5,7},{6,22},{7,5},{8,24},{9,11},... | collective-permute-start | bytes 1179656 | tf_op jit(solution)/shard_map/ppermute | solution.py:225
  8.9 7.1 %collective-permute-done.refs_1_ = bf16[48,4096]{1,0:T(8,128)(2,1)S(1)} collective-permute-done((bf16[48,4096]{1,0:T(8,128)(2,1)}, bf16[48,4096]{1,0:T(8,128)(2,1)S(1)}, u32[]{:S(2)}, u32[]{:S(2)}) %collective-permute-start) | collective-permute-done | bytes 393248 | tf_op jit(solution)/shard_map/ppermute | solution.py:225
  15.9 1.5 %collective-permute-start.15 = (bf16[48,4096]{1,0:T(8,128)(2,1)S(1)}, bf16[48,4096]{1,0:T(8,128)(2,1)S(1)}, u32[]{:S(2)}, u32[]{:S(2)}) collective-permute-start(bf16[48,4096]{1,0:T(8,128)(2,1)S(1)} %collective-permute-done.refs_1_), channel_id=1, source_target_pairs={{0,2},{1,17},{2,0},{3,19},{4,6},{5,21},{6,4},{7,23},{8,10},{9,25},... | collective-permute-start | bytes 1179656 | tf_op jit(solution)/shard_map/ppermute | solution.py:225
  17.5 1.5 %collective-permute-start.1 = (bf16[48,4096]{1,0:T(8,128)(2,1)S(1)}, bf16[48,4096]{1,0:T(8,128)(2,1)S(1)}, u32[]{:S(2)}, u32[]{:S(2)}) collective-permute-start(bf16[48,4096]{1,0:T(8,128)(2,1)S(1)} %collective-permute-done.refs_1_), channel_id=1, source_target_pairs={{0,16},{1,3},{2,18},{3,1},{4,20},{5,7},{6,22},{7,5},{8,24},{9,11},... | collective-permute-start | bytes 1179656 | tf_op jit(solution)/shard_map/ppermute | solution.py:225
  19.5 7.6 %collective-permute-done.6.refs_1_ = bf16[48,4096]{1,0:T(8,128)(2,1)} collective-permute-done((bf16[48,4096]{1,0:T(8,128)(2,1)S(1)}, bf16[48,4096]{1,0:T(8,128)(2,1)}, u32[]{:S(2)}, u32[]{:S(2)}) %collective-permute-start.6) | collective-permute-done | bytes 393248 | tf_op jit(solution)/shard_map/ppermute | solution.py:225
  27.3 0.7 copy-done.5
  28.1 1.8 %collective-permute-start.11 = (bf16[48,4096]{1,0:T(8,128)(2,1)S(1)}, bf16[48,4096]{1,0:T(8,128)(2,1)}, u32[]{:S(2)}, u32[]{:S(2)}) collective-permute-start(bf16[48,4096]{1,0:T(8,128)(2,1)S(1)} %collective-permute-done.3.refs_0_), channel_id=1, source_target_pairs={{0,4},{1,13},{2,6},{3,15},{4,0},{5,9},{6,2},{7,11},{8,12},{9,5},{1... | collective-permute-start | bytes 1179656 | tf_op jit(solution)/shard_map/ppermute | solution.py:225
  29.9 0.8 copy-done.3
  30.7 1.5 %collective-permute-start.7 = (bf16[48,4096]{1,0:T(8,128)(2,1)}, bf16[48,4096]{1,0:T(8,128)(2,1)}, u32[]{:S(2)}, u32[]{:S(2)}) collective-permute-start(bf16[48,4096]{1,0:T(8,128)(2,1)} %collective-permute-done.6.refs_1_), channel_id=1, source_target_pairs={{0,2},{1,17},{2,0},{3,19},{4,6},{5,21},{6,4},{7,23},{8,10},{9,25},... | collective-permute-start | bytes 1179656 | tf_op jit(solution)/shard_map/ppermute | solution.py:225
  32.2 1.5 %collective-permute-start.10 = (bf16[48,4096]{1,0:T(8,128)(2,1)}, bf16[48,4096]{1,0:T(8,128)(2,1)}, u32[]{:S(2)}, u32[]{:S(2)}) collective-permute-start(bf16[48,4096]{1,0:T(8,128)(2,1)} %collective-permute-done.6.refs_1_), channel_id=1, source_target_pairs={{0,16},{1,3},{2,18},{3,1},{4,20},{5,7},{6,22},{7,5},{8,24},{9,11},... | collective-permute-start | bytes 1179656 | tf_op jit(solution)/shard_map/ppermute | solution.py:225
  33.7 5.6 %collective-permute-done.13.refs_2_ = bf16[48,4096]{1,0:T(8,128)(2,1)} collective-permute-done((bf16[48,4096]{1,0:T(8,128)(2,1)S(1)}, bf16[48,4096]{1,0:T(8,128)(2,1)}, u32[]{:S(2)}, u32[]{:S(2)}) %collective-permute-start.13) | collective-permute-done | bytes 393248 | tf_op jit(solution)/shard_map/ppermute | solution.py:225
  39.4 1.5 %collective-permute-start.14 = (bf16[48,4096]{1,0:T(8,128)(2,1)}, bf16[48,4096]{1,0:T(8,128)(2,1)}, u32[]{:S(2)}, u32[]{:S(2)}) collective-permute-start(bf16[48,4096]{1,0:T(8,128)(2,1)} %collective-permute-done.13.refs_2_), channel_id=1, source_target_pairs={{0,2},{1,17},{2,0},{3,19},{4,6},{5,21},{6,4},{7,23},{8,10},{9,25},... | collective-permute-start | bytes 1179656 | tf_op jit(solution)/shard_map/ppermute | solution.py:225
  40.9 6.7 %collective-permute-done.11.refs_2_ = bf16[48,4096]{1,0:T(8,128)(2,1)} collective-permute-done((bf16[48,4096]{1,0:T(8,128)(2,1)S(1)}, bf16[48,4096]{1,0:T(8,128)(2,1)}, u32[]{:S(2)}, u32[]{:S(2)}) %collective-permute-start.11) | collective-permute-done | bytes 393248 | tf_op jit(solution)/shard_map/ppermute | solution.py:225
  47.6 1.5 %collective-permute-start.2 = (bf16[48,4096]{1,0:T(8,128)(2,1)}, bf16[48,4096]{1,0:T(8,128)(2,1)}, u32[]{:S(2)}, u32[]{:S(2)}) collective-permute-start(bf16[48,4096]{1,0:T(8,128)(2,1)} %copy-done.3), channel_id=1, source_target_pairs={{0,2},{1,17},{2,0},{3,19},{4,6},{5,21},{6,4},{7,23},{8,10},{9,25},... | collective-permute-start | bytes 1179656 | tf_op jit(solution)/shard_map/ppermute | solution.py:225
  49.1 1.6 %collective-permute-start.8 = (bf16[48,4096]{1,0:T(8,128)(2,1)}, bf16[48,4096]{1,0:T(8,128)(2,1)}, u32[]{:S(2)}, u32[]{:S(2)}) collective-permute-start(bf16[48,4096]{1,0:T(8,128)(2,1)} %collective-permute-done.7.refs_0_), channel_id=1, source_target_pairs={{0,16},{1,3},{2,18},{3,1},{4,20},{5,7},{6,22},{7,5},{8,24},{9,11},... | collective-permute-start | bytes 1179656 | tf_op jit(solution)/shard_map/ppermute | solution.py:225
  50.7 0.8 reshape.17.refs_5_.refs_6_
  52.2 1.6 %copy-done = bf16[256,4096]{1,0:T(8,128)(2,1)S(1)} copy-done((bf16[256,4096]{1,0:T(8,128)(2,1)S(1)}, bf16[256,4096]{1,0:T(8,128)(2,1)}, u32[]{:S(2)}) %copy-start) | copy-done | bytes 2097176
  53.8 1.0 %copy-done.2 = bf16[48,4096]{1,0:T(8,128)(2,1)S(1)} copy-done((bf16[48,4096]{1,0:T(8,128)(2,1)S(1)}, bf16[48,4096]{1,0:T(8,128)(2,1)}, u32[]{:S(2)}) %copy-start.2) | copy-done | bytes 393240
  54.8 2.0 %score.5.refs_6_ = f32[32,48]{1,0:T(8,128)S(1)} custom-call(s32[16]{0:T(128)S(1)} %get-tuple-element.7.slot_ref, s32[16]{0:T(128)S(1)} %get-tuple-element.6.dev_ref, s32[2]{0:T(128)S(1)} %pad_add_fusion.base_ref, bf16[48,4096]{1,0:T(8,128)(2,1)S(1)} %copy-done.2, bf16[48,4096]{1,0:T(8,128)(2,1)S(1)} %collective-permute-done.refs_1_, ...), custom_call_target="tpu_custom_call" | custom-call | flops 603979776 | bytes 5373952 | tf_op jit(solution)/shard_map/score/pallas_call | solution.py:141
  56.8 2.5 %score.6.refs_6_ = f32[32,48]{1,0:T(8,128)S(1)} custom-call(s32[16]{0:T(128)S(1)} %get-tuple-element.7.slot_ref, s32[16]{0:T(128)S(1)} %get-tuple-element.6.dev_ref, s32[2]{0:T(128)S(1)} %pad_add_fusion.base_ref, bf16[48,4096]{1,0:T(8,128)(2,1)S(1)} %collective-permute-done.3.refs_0_, bf16[48,4096]{1,0:T(8,128)(2,1)} %collective-permute-done.6.refs_1_, ...), custom_call_target="tpu_custom_call" | custom-call | flops 603979776 | bytes 5373952 | tf_op jit(solution)/shard_map/score/pallas_call | solution.py:141
  59.3 2.6 %score.7.refs_7_ = f32[32,48]{1,0:T(8,128)S(1)} custom-call(s32[16]{0:T(128)S(1)} %get-tuple-element.7.slot_ref, s32[16]{0:T(128)S(1)} %get-tuple-element.6.dev_ref, s32[2]{0:T(128)S(1)} %pad_add_fusion.base_ref, bf16[48,4096]{1,0:T(8,128)(2,1)S(1)} %copy-done.4, bf16[48,4096]{1,0:T(8,128)(2,1)} %collective-permute-done.4.refs_1_, ...), custom_call_target="tpu_custom_call" | custom-call | flops 603979776 | bytes 5373952 | tf_op jit(solution)/shard_map/score/pallas_call | solution.py:141
  62.0 2.8 %score.8.refs_6_ = f32[32,48]{1,0:T(8,128)S(1)} custom-call(s32[16]{0:T(128)S(1)} %get-tuple-element.7.slot_ref, s32[16]{0:T(128)S(1)} %get-tuple-element.6.dev_ref, s32[2]{0:T(128)S(1)} %pad_add_fusion.base_ref, bf16[48,4096]{1,0:T(8,128)(2,1)} %collective-permute-done.7.refs_0_, bf16[48,4096]{1,0:T(8,128)(2,1)} %collective-permute-done.10.refs_1_, ...), custom_call_target="tpu_custom_call" | custom-call | flops 805306368 | bytes 5767168 | tf_op jit(solution)/shard_map/score/pallas_call | solution.py:141
  64.8 2.7 %score.9 = f32[32,48]{1,0:T(8,128)S(1)} custom-call(s32[16]{0:T(128)S(1)} %get-tuple-element.7.slot_ref, s32[16]{0:T(128)S(1)} %get-tuple-element.6.dev_ref, s32[2]{0:T(128)S(1)} %pad_add_fusion.base_ref, bf16[48,4096]{1,0:T(8,128)(2,1)} %collective-permute-done.2.refs_0_, bf16[48,4096]{1,0:T(8,128)(2,1)} %collective-permute-done.5.refs_1_, ...), custom_call_target="tpu_custom_call" | custom-call | flops 603979776 | bytes 5373952 | tf_op jit(solution)/shard_map/score/pallas_call | solution.py:141
  67.5 2.0 %collective-permute-start.16 = (f32[32,48]{1,0:T(8,128)S(1)}, f32[32,48]{1,0:T(8,128)S(1)}, u32[]{:S(2)}, u32[]{:S(2)}) collective-permute-start(f32[32,48]{1,0:T(8,128)S(1)} %score.9), channel_id=1, source_target_pairs={{0,4},{1,5},{2,6},{3,7},{4,0},{5,1},{6,2},{7,3},{8,12},{9,13},{10,... | collective-permute-start | bytes 18440 | tf_op jit(solution)/shard_map/ppermute | solution.py:225
  70.0 2.0 %collective-permute-start.18 = (f32[32,48]{1,0:T(8,128)S(1)}, f32[32,48]{1,0:T(8,128)S(1)}, u32[]{:S(2)}, u32[]{:S(2)}) collective-permute-start(f32[32,48]{1,0:T(8,128)S(1)} %score.9), channel_id=1, source_target_pairs={{0,12},{1,13},{2,14},{3,15},{4,8},{5,9},{6,10},{7,11},{8,4},{9,5},... | collective-permute-start | bytes 18440 | tf_op jit(solution)/shard_map/ppermute | solution.py:225
  71.9 2.2 %collective-permute-done.17 = f32[32,48]{1,0:T(8,128)S(1)} collective-permute-done((f32[32,48]{1,0:T(8,128)S(1)}, f32[32,48]{1,0:T(8,128)S(1)}, u32[]{:S(2)}, u32[]{:S(2)}) %collective-permute-start.17) | collective-permute-done | bytes 6176 | tf_op jit(solution)/shard_map/ppermute | solution.py:225
  74.1 1.4 %collective-permute-done.18 = f32[32,48]{1,0:T(8,128)S(1)} collective-permute-done((f32[32,48]{1,0:T(8,128)S(1)}, f32[32,48]{1,0:T(8,128)S(1)}, u32[]{:S(2)}, u32[]{:S(2)}) %collective-permute-start.18) | collective-permute-done | bytes 6176 | tf_op jit(solution)/shard_map/ppermute | solution.py:225
  76.6 2.5 %collective-permute-start.21 = (f32[32,48]{1,0:T(8,128)S(1)}, f32[32,48]{1,0:T(8,128)S(1)}, u32[]{:S(2)}, u32[]{:S(2)}) collective-permute-start(f32[32,48]{1,0:T(8,128)S(1)} %pad_maximum_fusion), channel_id=1, source_target_pairs={{0,18},{1,19},{2,16},{3,17},{4,22},{5,23},{6,20},{7,21},{8,26},{9,... | collective-permute-start | bytes 18440 | tf_op jit(solution)/shard_map/ppermute | solution.py:225
  79.8 1.4 %collective-permute-done.21 = f32[32,48]{1,0:T(8,128)S(1)} collective-permute-done((f32[32,48]{1,0:T(8,128)S(1)}, f32[32,48]{1,0:T(8,128)S(1)}, u32[]{:S(2)}, u32[]{:S(2)}) %collective-permute-start.21) | collective-permute-done | bytes 6176 | tf_op jit(solution)/shard_map/ppermute | solution.py:225
  81.4 1.2 %collective-permute-done.22.theirs = f32[16,48]{1,0:T(8,128)S(1)} collective-permute-done((f32[16,48]{1,0:T(8,128)S(1)}, f32[16,48]{1,0:T(8,128)S(1)}, u32[]{:S(2)}, u32[]{:S(2)}) %collective-permute-start.22) | collective-permute-done | bytes 3104 | tf_op jit(solution)/shard_map/ppermute | solution.py:225
  (41 shorter events, 5.3 us)
Async XLA Ops:
  0.6 48.5 %collective-permute-start.9 = (bf16[256,4096]{1,0:T(8,128)(2,1)}, bf16[256,4096]{1,0:T(8,128)(2,1)S(1)}, u32[]{:S(2)}, u32[]{:S(2)}) collective-permute-start(bf16[256,4096]{1,0:T(8,128)(2,1)} %refs_3_.7), channel_id=1, source_target_pairs={{0,1},{1,0},{2,3},{3,2},{4,5},{5,4},{6,7},{7,6},{8,9},{9,8},{10,11... | collective-permute-start | bytes 6291464 | tf_op jit(solution)/shard_map/ppermute | solution.py:225
  1.2 14.7 %collective-permute-start = (bf16[48,4096]{1,0:T(8,128)(2,1)}, bf16[48,4096]{1,0:T(8,128)(2,1)S(1)}, u32[]{:S(2)}, u32[]{:S(2)}) collective-permute-start(bf16[48,4096]{1,0:T(8,128)(2,1)} %refs_0_.1), channel_id=1, source_target_pairs={{0,12},{1,5},{2,14},{3,7},{4,8},{5,1},{6,10},{7,3},{8,4},{9,13},{1... | collective-permute-start | bytes 1179656 | tf_op jit(solution)/shard_map/ppermute | solution.py:225
  5.9 11.6 %collective-permute-start.12 = (bf16[48,4096]{1,0:T(8,128)(2,1)}, bf16[48,4096]{1,0:T(8,128)(2,1)S(1)}, u32[]{:S(2)}, u32[]{:S(2)}) collective-permute-start(bf16[48,4096]{1,0:T(8,128)(2,1)} %refs_0_.1), channel_id=1, source_target_pairs={{0,2},{1,17},{2,0},{3,19},{4,6},{5,21},{6,4},{7,23},{8,10},{9,25},... | collective-permute-start | bytes 1179656 | tf_op jit(solution)/shard_map/ppermute | solution.py:225
  7.4 11.6 %collective-permute-start.3 = (bf16[48,4096]{1,0:T(8,128)(2,1)}, bf16[48,4096]{1,0:T(8,128)(2,1)S(1)}, u32[]{:S(2)}, u32[]{:S(2)}) collective-permute-start(bf16[48,4096]{1,0:T(8,128)(2,1)} %refs_0_.1), channel_id=1, source_target_pairs={{0,16},{1,3},{2,18},{3,1},{4,20},{5,7},{6,22},{7,5},{8,24},{9,11},... | collective-permute-start | bytes 1179656 | tf_op jit(solution)/shard_map/ppermute | solution.py:225
  15.9 11.2 %collective-permute-start.6 = (bf16[48,4096]{1,0:T(8,128)(2,1)S(1)}, bf16[48,4096]{1,0:T(8,128)(2,1)}, u32[]{:S(2)}, u32[]{:S(2)}) collective-permute-start(bf16[48,4096]{1,0:T(8,128)(2,1)S(1)} %collective-permute-done.refs_1_), channel_id=1, source_target_pairs={{0,4},{1,13},{2,6},{3,15},{4,0},{5,9},{6,2},{7,11},{8,12},{9,5},{1... | collective-permute-start | bytes 1179656 | tf_op jit(solution)/shard_map/ppermute | solution.py:225
  15.9 11.4 %collective-permute-start.15 = (bf16[48,4096]{1,0:T(8,128)(2,1)S(1)}, bf16[48,4096]{1,0:T(8,128)(2,1)S(1)}, u32[]{:S(2)}, u32[]{:S(2)}) collective-permute-start(bf16[48,4096]{1,0:T(8,128)(2,1)S(1)} %collective-permute-done.refs_1_), channel_id=1, source_target_pairs={{0,2},{1,17},{2,0},{3,19},{4,6},{5,21},{6,4},{7,23},{8,10},{9,25},... | collective-permute-start | bytes 1179656 | tf_op jit(solution)/shard_map/ppermute | solution.py:225
  17.5 12.4 %collective-permute-start.1 = (bf16[48,4096]{1,0:T(8,128)(2,1)S(1)}, bf16[48,4096]{1,0:T(8,128)(2,1)S(1)}, u32[]{:S(2)}, u32[]{:S(2)}) collective-permute-start(bf16[48,4096]{1,0:T(8,128)(2,1)S(1)} %collective-permute-done.refs_1_), channel_id=1, source_target_pairs={{0,16},{1,3},{2,18},{3,1},{4,20},{5,7},{6,22},{7,5},{8,24},{9,11},... | collective-permute-start | bytes 1179656 | tf_op jit(solution)/shard_map/ppermute | solution.py:225
  19.0 13.3 %collective-permute-start.4 = (bf16[48,4096]{1,0:T(8,128)(2,1)S(1)}, bf16[48,4096]{1,0:T(8,128)(2,1)}, u32[]{:S(2)}, u32[]{:S(2)}) collective-permute-start(bf16[48,4096]{1,0:T(8,128)(2,1)S(1)} %collective-permute-done.3.refs_0_), channel_id=1, source_target_pairs={{0,2},{1,17},{2,0},{3,19},{4,6},{5,21},{6,4},{7,23},{8,10},{9,25},... | collective-permute-start | bytes 1179656 | tf_op jit(solution)/shard_map/ppermute | solution.py:225
  27.1 12.2 %collective-permute-start.13 = (bf16[48,4096]{1,0:T(8,128)(2,1)S(1)}, bf16[48,4096]{1,0:T(8,128)(2,1)}, u32[]{:S(2)}, u32[]{:S(2)}) collective-permute-start(bf16[48,4096]{1,0:T(8,128)(2,1)S(1)} %collective-permute-done.12.refs_2_), channel_id=1, source_target_pairs={{0,4},{1,13},{2,6},{3,15},{4,0},{5,9},{6,2},{7,11},{8,12},{9,5},{1... | collective-permute-start | bytes 1179656 | tf_op jit(solution)/shard_map/ppermute | solution.py:225
  27.3 0.7 copy-start.5
  28.1 19.5 %collective-permute-start.11 = (bf16[48,4096]{1,0:T(8,128)(2,1)S(1)}, bf16[48,4096]{1,0:T(8,128)(2,1)}, u32[]{:S(2)}, u32[]{:S(2)}) collective-permute-start(bf16[48,4096]{1,0:T(8,128)(2,1)S(1)} %collective-permute-done.3.refs_0_), channel_id=1, source_target_pairs={{0,4},{1,13},{2,6},{3,15},{4,0},{5,9},{6,2},{7,11},{8,12},{9,5},{1... | collective-permute-start | bytes 1179656 | tf_op jit(solution)/shard_map/ppermute | solution.py:225
  29.9 0.8 copy-start.3
  30.7 18.4 %collective-permute-start.7 = (bf16[48,4096]{1,0:T(8,128)(2,1)}, bf16[48,4096]{1,0:T(8,128)(2,1)}, u32[]{:S(2)}, u32[]{:S(2)}) collective-permute-start(bf16[48,4096]{1,0:T(8,128)(2,1)} %collective-permute-done.6.refs_1_), channel_id=1, source_target_pairs={{0,2},{1,17},{2,0},{3,19},{4,6},{5,21},{6,4},{7,23},{8,10},{9,25},... | collective-permute-start | bytes 1179656 | tf_op jit(solution)/shard_map/ppermute | solution.py:225
  32.2 29.7 %collective-permute-start.10 = (bf16[48,4096]{1,0:T(8,128)(2,1)}, bf16[48,4096]{1,0:T(8,128)(2,1)}, u32[]{:S(2)}, u32[]{:S(2)}) collective-permute-start(bf16[48,4096]{1,0:T(8,128)(2,1)} %collective-permute-done.6.refs_1_), channel_id=1, source_target_pairs={{0,16},{1,3},{2,18},{3,1},{4,20},{5,7},{6,22},{7,5},{8,24},{9,11},... | collective-permute-start | bytes 1179656 | tf_op jit(solution)/shard_map/ppermute | solution.py:225
  39.4 22.6 %collective-permute-start.14 = (bf16[48,4096]{1,0:T(8,128)(2,1)}, bf16[48,4096]{1,0:T(8,128)(2,1)}, u32[]{:S(2)}, u32[]{:S(2)}) collective-permute-start(bf16[48,4096]{1,0:T(8,128)(2,1)} %collective-permute-done.13.refs_2_), channel_id=1, source_target_pairs={{0,2},{1,17},{2,0},{3,19},{4,6},{5,21},{6,4},{7,23},{8,10},{9,25},... | collective-permute-start | bytes 1179656 | tf_op jit(solution)/shard_map/ppermute | solution.py:225
  47.6 17.2 %collective-permute-start.2 = (bf16[48,4096]{1,0:T(8,128)(2,1)}, bf16[48,4096]{1,0:T(8,128)(2,1)}, u32[]{:S(2)}, u32[]{:S(2)}) collective-permute-start(bf16[48,4096]{1,0:T(8,128)(2,1)} %copy-done.3), channel_id=1, source_target_pairs={{0,2},{1,17},{2,0},{3,19},{4,6},{5,21},{6,4},{7,23},{8,10},{9,25},... | collective-permute-start | bytes 1179656 | tf_op jit(solution)/shard_map/ppermute | solution.py:225
  49.1 15.7 %collective-permute-start.5 = (bf16[48,4096]{1,0:T(8,128)(2,1)}, bf16[48,4096]{1,0:T(8,128)(2,1)}, u32[]{:S(2)}, u32[]{:S(2)}) collective-permute-start(bf16[48,4096]{1,0:T(8,128)(2,1)} %collective-permute-done.4.refs_1_), channel_id=1, source_target_pairs={{0,4},{1,13},{2,6},{3,15},{4,0},{5,9},{6,2},{7,11},{8,12},{9,5},{1... | collective-permute-start | bytes 1179656 | tf_op jit(solution)/shard_map/ppermute | solution.py:225
  49.1 15.7 %collective-permute-start.8 = (bf16[48,4096]{1,0:T(8,128)(2,1)}, bf16[48,4096]{1,0:T(8,128)(2,1)}, u32[]{:S(2)}, u32[]{:S(2)}) collective-permute-start(bf16[48,4096]{1,0:T(8,128)(2,1)} %collective-permute-done.7.refs_0_), channel_id=1, source_target_pairs={{0,16},{1,3},{2,18},{3,1},{4,20},{5,7},{6,22},{7,5},{8,24},{9,11},... | collective-permute-start | bytes 1179656 | tf_op jit(solution)/shard_map/ppermute | solution.py:225
  52.2 1.6 %copy-start = (bf16[256,4096]{1,0:T(8,128)(2,1)S(1)}, bf16[256,4096]{1,0:T(8,128)(2,1)}, u32[]{:S(2)}) copy-start(bf16[256,4096]{1,0:T(8,128)(2,1)} %refs_3_.7) | copy-start | bytes 6291460
  53.8 1.0 %copy-start.2 = (bf16[48,4096]{1,0:T(8,128)(2,1)S(1)}, bf16[48,4096]{1,0:T(8,128)(2,1)}, u32[]{:S(2)}) copy-start(bf16[48,4096]{1,0:T(8,128)(2,1)} %refs_0_.1) | copy-start | bytes 1179652
  54.8 2.0 %copy-start.1 = (bf16[256,4096]{1,0:T(8,128)(2,1)S(1)}, bf16[256,4096]{1,0:T(8,128)(2,1)}, u32[]{:S(2)}) copy-start(bf16[256,4096]{1,0:T(8,128)(2,1)} %refs_3_.7) | copy-start | bytes 6291460
  54.8 2.0 %copy-start.6 = (bf16[48,4096]{1,0:T(8,128)(2,1)S(1)}, bf16[48,4096]{1,0:T(8,128)(2,1)}, u32[]{:S(2)}) copy-start(bf16[48,4096]{1,0:T(8,128)(2,1)} %copy-done.5) | copy-start | bytes 1179652
  56.8 2.5 %copy-start.4 = (bf16[48,4096]{1,0:T(8,128)(2,1)S(1)}, bf16[48,4096]{1,0:T(8,128)(2,1)}, u32[]{:S(2)}) copy-start(bf16[48,4096]{1,0:T(8,128)(2,1)} %copy-done.3) | copy-start | bytes 1179652
  67.5 4.4 %collective-permute-start.16 = (f32[32,48]{1,0:T(8,128)S(1)}, f32[32,48]{1,0:T(8,128)S(1)}, u32[]{:S(2)}, u32[]{:S(2)}) collective-permute-start(f32[32,48]{1,0:T(8,128)S(1)} %score.9), channel_id=1, source_target_pairs={{0,4},{1,5},{2,6},{3,7},{4,0},{5,1},{6,2},{7,3},{8,12},{9,13},{10,... | collective-permute-start | bytes 18440 | tf_op jit(solution)/shard_map/ppermute | solution.py:225
  69.5 4.6 %collective-permute-start.17 = (f32[32,48]{1,0:T(8,128)S(1)}, f32[32,48]{1,0:T(8,128)S(1)}, u32[]{:S(2)}, u32[]{:S(2)}) collective-permute-start(f32[32,48]{1,0:T(8,128)S(1)} %score.9), channel_id=1, source_target_pairs={{0,8},{1,9},{2,10},{3,11},{4,12},{5,13},{6,14},{7,15},{8,0},{9,1},... | collective-permute-start | bytes 18440 | tf_op jit(solution)/shard_map/ppermute | solution.py:225
  70.0 5.5 %collective-permute-start.18 = (f32[32,48]{1,0:T(8,128)S(1)}, f32[32,48]{1,0:T(8,128)S(1)}, u32[]{:S(2)}, u32[]{:S(2)}) collective-permute-start(f32[32,48]{1,0:T(8,128)S(1)} %score.9), channel_id=1, source_target_pairs={{0,12},{1,13},{2,14},{3,15},{4,8},{5,9},{6,10},{7,11},{8,4},{9,5},... | collective-permute-start | bytes 18440 | tf_op jit(solution)/shard_map/ppermute | solution.py:225
  75.5 3.8 %collective-permute-start.19 = (f32[32,48]{1,0:T(8,128)S(1)}, f32[32,48]{1,0:T(8,128)S(1)}, u32[]{:S(2)}, u32[]{:S(2)}) collective-permute-start(f32[32,48]{1,0:T(8,128)S(1)} %pad_maximum_fusion), channel_id=1, source_target_pairs={{0,2},{1,3},{2,0},{3,1},{4,6},{5,7},{6,4},{7,5},{8,10},{9,11},{10,... | collective-permute-start | bytes 18440 | tf_op jit(solution)/shard_map/ppermute | solution.py:225
  76.1 3.7 %collective-permute-start.20 = (f32[32,48]{1,0:T(8,128)S(1)}, f32[32,48]{1,0:T(8,128)S(1)}, u32[]{:S(2)}, u32[]{:S(2)}) collective-permute-start(f32[32,48]{1,0:T(8,128)S(1)} %pad_maximum_fusion), channel_id=1, source_target_pairs={{0,16},{1,17},{2,18},{3,19},{4,20},{5,21},{6,22},{7,23},{8,24},{9,... | collective-permute-start | bytes 18440 | tf_op jit(solution)/shard_map/ppermute | solution.py:225
  76.6 4.6 %collective-permute-start.21 = (f32[32,48]{1,0:T(8,128)S(1)}, f32[32,48]{1,0:T(8,128)S(1)}, u32[]{:S(2)}, u32[]{:S(2)}) collective-permute-start(f32[32,48]{1,0:T(8,128)S(1)} %pad_maximum_fusion), channel_id=1, source_target_pairs={{0,18},{1,19},{2,16},{3,17},{4,22},{5,23},{6,20},{7,21},{8,26},{9,... | collective-permute-start | bytes 18440 | tf_op jit(solution)/shard_map/ppermute | solution.py:225
  81.3 1.2 %collective-permute-start.22 = (f32[16,48]{1,0:T(8,128)S(1)}, f32[16,48]{1,0:T(8,128)S(1)}, u32[]{:S(2)}, u32[]{:S(2)}) collective-permute-start(f32[16,48]{1,0:T(8,128)S(1)} %fusion.1.mine), channel_id=1, source_target_pairs={{0,1},{1,0},{2,3},{3,2},{4,5},{5,4},{6,7},{7,6},{8,9},{9,8},{10,11... | collective-permute-start | bytes 9224 | tf_op jit(solution)/shard_map/ppermute | solution.py:225
